TPU v7x, 32 devices: a whole 2x2x4 slice. The times are simulated.
32 devices in a mesh: groups: 2 (over y), res: 8 (over z, x), seq: 2 (over core).
Axes of the slice: x: 2, y: 2, z: 4, core: 2. Of those that a mesh axis runs over, the one named last changes fastest.
Arguments:
- alignment: bfloat16 [128, 32, 256], P(('groups', 'seq'), 'res'), parts along dimension 0, may hold values from -6 to 6
- ln_gain: float32 [256], replicated, may hold values from 0.1 to 1.9
- proj_left: bfloat16 [256, 32], replicated, may hold values from -0.375 to 0.375
- proj_right: bfloat16 [256, 32], replicated, may hold values from -0.375 to 0.375
- out_weight: bfloat16 [1024, 128], replicated, may hold values from -4 to 4
- out_bias: float32 [128], replicated, may hold values from -3 to 3
Outputs:
- pair_update: bfloat16 [64, 32, 128], P(('groups', 'res'), 'seq'), parts along dimension 0
There are 2 independent parts, one for each index of `groups`. A program takes and returns all parts, laid end to end along the dimension named above; an argument that names none is the same for every part. Nothing has to cross between parts.
All inputs are finite; a program needn't handle non-finite values.
Results may differ from a plain program's by a relative error of at most 0.0095.
Values may be sent and summed in bfloat16 or wider, within the bound.
No kernel may reach another device: no remote copies, remote signals or barrier semaphores. Data moves between devices by JAX's collectives and lax.ppermute only.
A program may use at most 64 MiB of HBM per device.

v0:
```python
import math

import jax
import jax.numpy as jnp
from jax import lax
from jax.sharding import PartitionSpec as P


def normalize(alignment, ln_gain):
    values = alignment.astype(jnp.float32)
    centred = values - jnp.mean(values, axis=-1, keepdims=True)
    variance = jnp.mean(centred * centred, axis=-1, keepdims=True)
    return (centred * lax.rsqrt(variance + 1e-05) * ln_gain).astype(jnp.bfloat16)


def pair_block(left_flat, columns, weight_full, inv_count):
    channels = columns.shape[2]
    col_count = columns.shape[1]
    row_count = left_flat.shape[1] // channels
    block_width = math.gcd(col_count, 64)

    def advance(position, totals):
        column_block = lax.dynamic_slice_in_dim(columns, position * block_width, block_width, 1)
        right_flat = column_block.reshape(columns.shape[0], block_width * channels)
        outer_terms = (
            lax.dot_general(
                left_flat, right_flat, (((0,), (0,)), ((), ())), preferred_element_type=jnp.float32
            )
            * inv_count
        )
        outer_terms = outer_terms.reshape(row_count, channels, block_width, channels).transpose(
            0, 2, 1, 3
        )
        outer_terms = outer_terms.reshape(row_count * block_width, channels * channels)
        projected = jnp.dot(outer_terms, weight_full, precision=lax.Precision.HIGHEST)
        projected = projected.reshape(row_count, block_width, weight_full.shape[1])
        return lax.dynamic_update_slice_in_dim(totals, projected, position * block_width, 1)

    totals = jnp.zeros((row_count, col_count, weight_full.shape[1]), jnp.float32)
    return lax.fori_loop(0, col_count // block_width, advance, totals)


def on_device(alignment, ln_gain, proj_left, proj_right, out_weight, out_bias):
    seq_shards = lax.axis_size("seq")
    local_seqs = alignment.shape[0]
    local_res = alignment.shape[1]
    channels = proj_left.shape[1]
    inv_count = 1.0 / (local_seqs * seq_shards)
    normed = normalize(alignment, ln_gain)
    flat_rows = normed.reshape(-1, normed.shape[2])
    both_sides = jnp.dot(
        flat_rows, jnp.concatenate((proj_left, proj_right), 1), preferred_element_type=jnp.float32
    )
    both_sides = both_sides.astype(jnp.bfloat16).reshape(local_seqs, local_res, 2 * channels)
    left_side = both_sides[:, :, :channels]
    right_side = both_sides[:, :, channels:]
    weight_full = out_weight.astype(jnp.float32)
    left_all = lax.all_gather(left_side, "seq", axis=0, tiled=True)
    left_flat = left_all.reshape(left_all.shape[0], local_res * channels)
    right_all = lax.all_gather(right_side, "res", axis=1, tiled=True)
    split_right = right_all.reshape(
        local_seqs, seq_shards, right_all.shape[1] // seq_shards, channels
    )
    arrived = lax.all_to_all(split_right, "seq", split_axis=1, concat_axis=0, tiled=True)
    squeezed = arrived.reshape(arrived.shape[0], arrived.shape[2], arrived.shape[3])
    summed = pair_block(left_flat, squeezed, weight_full, inv_count)
    return (summed + out_bias).astype(jnp.bfloat16)


def solution(mesh):
    placed = (P(("groups", "seq"), "res", None), P(), P(), P(), P(), P())
    return jax.shard_map(
        on_device,
        mesh=mesh,
        in_specs=placed,
        out_specs=P(("groups", "res"), "seq", None),
        check_vma=False,
    )
```

profile of v0, /device:TPU:0, one launch (start us, length us, event | category | flops | bytes accessed | tf_op | source)
XLA Modules:
  0.0 44.9 jit_solution(8482532180802499849)
XLA Ops:
  0.0 0.0 copy-start
  0.0 0.0 copy-start.1
  0.0 1.0 %convert_reduce_fusion = f32[32,4]{1,0:T(8,128)S(1)} fusion(bf16[32,4,256]{2,1,0:T(4,128)(2,1)} %param.6), kind=kLoop, calls=%fused_computation.6 | loop fusion | flops 65408 | bytes 66048 | tf_op jit(solution)/shard_map/reduce_sum | solution.py:11
  1.0 0.0 copy-done.1
  1.1 0.2 fusion.4
  1.2 0.0 copy-start.4
  1.3 0.7 %copy-done.4 = f32[256]{0:T(256)S(1)} copy-done((f32[256]{0:T(256)S(1)}, f32[256]{0:T(256)}, u32[]{:S(2)}) %copy-start.4) | copy-done | bytes 1048
  1.9 0.1 fusion.6
  2.1 0.0 copy-start.2
  2.1 0.0 copy-start.3
  2.1 0.7 %copy-done.2 = bf16[256,32]{0,1:T(8,128)(2,1)S(1)} copy-done((bf16[256,32]{0,1:T(8,128)(2,1)S(1)}, bf16[256,32]{0,1:T(8,128)(2,1)}, u32[]{:S(2)}) %copy-start.2) | copy-done | bytes 16408
  2.8 0.0 copy-done.3
  2.8 0.1 convolution_convert_fusion
  2.9 0.1 copy.12
  3.1 0.1 fusion.11
  3.2 32.6 %all_gather.7 = bf16[32,32,32]{2,0,1:T(8,128)(2,1)S(1)} all-gather(bf16[32,4,32]{2,0,1:T(8,128)(2,1)S(1)} %copy.14), channel_id=1, replica_groups=mesh['groups'=2,'res'=8,'seq'=2] {'res'}, dimensions={1}, use_global_device_ids=true | all-gather | bytes 73728 | tf_op jit(solution)/shard_map/all_gather | solution.py:60
  35.7 0.1 copy.21
  35.9 0.9 %reshape.50 = bf16[2,2,8192]{2,1,0:T(2,128)(2,1)} reshape(bf16[2,32,16,32]{3,2,1,0:T(8,128)(2,1)S(1)} %bitcast.27) | data formatting | bytes 131072
  36.8 3.3 %all-to-all-start = ((bf16[2,2,8192]{2,1,0:T(2,128)(2,1)}), bf16[2,2,8192]{2,1,0:T(2,128)(2,1)S(1)}, u32[]{:S(2)}, u32[]{:S(2)}) async-start(bf16[2,2,8192]{2,1,0:T(2,128)(2,1)} %reshape.50), calls=%async_computation | async-start | bytes 131072 | tf_op jit(solution)/shard_map/all_to_all | solution.py:64
  40.1 2.0 %all_gather.6 = bf16[64,4,32]{2,1,0:T(4,128)(2,1)S(1)} all-gather(bf16[32,4,32]{2,1,0:T(4,128)(2,1)S(1)} %get-tuple-element.16), channel_id=1, replica_groups=mesh['groups'=2,'res'=8,'seq'=2] {'seq'}, dimensions={0}, use_global_device_ids=true | all-gather | bytes 24576 | tf_op jit(solution)/shard_map/all_gather | solution.py:58
  42.0 0.1 copy.13
  42.1 0.0 all-to-all-done
  42.2 0.2 reshape.51
  42.4 0.2 reshape.47
  42.6 0.2 convolution_multiply_fusion
  42.8 0.3 reshape.48
  43.1 0.3 copy.17
  43.4 0.0 copy-start.5
  43.4 0.5 %dot_general.15 = f32[4,16,1024]{2,1,0:T(8,128)S(1)} reshape(f32[4,16,32,32]{3,2,1,0:T(8,128)S(1)} %copy.17) | data formatting | bytes 524288 | tf_op jit(solution)/shard_map/while/body/eval_jaxpr/dot_general | solution.py:35
  43.9 0.0 copy-done
  43.9 0.1 copy-done.5
  44.0 0.9 %fusion = bf16[4,16,128]{2,1,0:T(8,128)(2,1)} fusion(f32[4,16,1024]{2,1,0:T(8,128)S(1)} %dot_general.15, bf16[1024,128]{1,0:T(8,128)(2,1)S(1)} %copy-done, f32[128]{0:T(128)S(1)} %copy-done.5), kind=kOutput, calls=%fused_computation.3 | convolution fusion | flops 100679680 | bytes 541184 | tf_op jit(solution)/shard_map/while/body/eval_jaxpr/dot_general | solution.py:35
  (5 shorter events, 0.1 us)
Async XLA Ops:
  0.0 43.9 %copy-start = (bf16[1024,128]{1,0:T(8,128)(2,1)S(1)}, bf16[1024,128]{1,0:T(8,128)(2,1)}, u32[]{:S(2)}) copy-start(bf16[1024,128]{1,0:T(8,128)(2,1)} %param.10) | copy-start | bytes 786436
  0.0 1.0 %copy-start.1 = (bf16[32,4,256]{2,1,0:T(4,128)(2,1)S(1)}, bf16[32,4,256]{2,1,0:T(4,128)(2,1)}, u32[]{:S(2)}) copy-start(bf16[32,4,256]{2,1,0:T(4,128)(2,1)} %param.6) | copy-start | bytes 196612
  1.2 0.7 %copy-start.4 = (f32[256]{0:T(256)S(1)}, f32[256]{0:T(256)}, u32[]{:S(2)}) copy-start(f32[256]{0:T(256)} %param.7) | copy-start | bytes 3076
  2.1 0.7 %copy-start.2 = (bf16[256,32]{0,1:T(8,128)(2,1)S(1)}, bf16[256,32]{0,1:T(8,128)(2,1)}, u32[]{:S(2)}) copy-start(bf16[256,32]{0,1:T(8,128)(2,1)} %param.9) | copy-start | bytes 49156
  2.1 0.7 %copy-start.3 = (bf16[256,32]{0,1:T(8,128)(2,1)S(1)}, bf16[256,32]{0,1:T(8,128)(2,1)}, u32[]{:S(2)}) copy-start(bf16[256,32]{0,1:T(8,128)(2,1)} %param.8) | copy-start | bytes 49156
  36.8 5.4 %all-to-all-start = ((bf16[2,2,8192]{2,1,0:T(2,128)(2,1)}), bf16[2,2,8192]{2,1,0:T(2,128)(2,1)S(1)}, u32[]{:S(2)}, u32[]{:S(2)}) async-start(bf16[2,2,8192]{2,1,0:T(2,128)(2,1)} %reshape.50), calls=%async_computation | async-start | bytes 131072 | tf_op jit(solution)/shard_map/all_to_all | solution.py:64
  43.4 0.7 %copy-start.5 = (f32[128]{0:T(128)S(1)}, f32[128]{0:T(128)}, u32[]{:S(2)}) copy-start(f32[128]{0:T(128)} %param.11) | copy-start | bytes 1540
where the time goes:
time: 45.3 us; the launch traced here: 44.9 us
  blocking collectives  34.5 us (76%)
  local copies, waits for them, and re-layouts  4.41 us (10%)
  starting transfers between devices  3.29 us (7%)
  other arithmetic  1.34 us (3%)
  matrix products  1.15 us (3%)
    all_gather x1, blocking collectives, on_device(): right_all = lax.all_gather(right_side, 'res', axis=1, tiled=True)  32.6 us
    all_to_all x1, starting transfers between devices, on_device(): lax.all_to_all(split_right, 'seq', split_axis=1, concat_axis=0, tiled=True)  3.29 us
    unnamed x14, local copies, waits for them, and re-layouts  2.61 us
    all_gather x1, blocking collectives, on_device(): left_all = lax.all_gather(left_side, 'seq', axis=0, tiled=True)  1.98 us
    reduce_sum x1, other arithmetic, normalize(): centred = values - jnp.mean(values, axis=-1, keepdims=True)  1.02 us
  transfers between devices with their start and end apart: 1, of which 0 were waited for; matrix products, arithmetic and copies ran while one was open for 0% of the time, Pallas kernels for 0%

commit v1 on v0

--- a/solution.py
+++ b/solution.py
@@ -1,10 +1,12 @@
+import functools
 import math
 
 import jax
 import jax.numpy as jnp
 from jax import lax
+from jax.experimental import pallas as pl
+from jax.experimental.pallas import tpu as pltpu
 from jax.sharding import PartitionSpec as P
-
 
 def normalize(alignment, ln_gain):
     values = alignment.astype(jnp.float32)
@@ -40,7 +42,7 @@
     return lax.fori_loop(0, col_count // block_width, advance, totals)
 
 
-def on_device(alignment, ln_gain, proj_left, proj_right, out_weight, out_bias):
+def gathered(alignment, ln_gain, proj_left, proj_right, out_weight, out_bias):
     seq_shards = lax.axis_size("seq")
     local_seqs = alignment.shape[0]
     local_res = alignment.shape[1]
@@ -67,10 +69,125 @@
     return (summed + out_bias).astype(jnp.bfloat16)
 
 
+VMEM = pl.BlockSpec(memory_space=pltpu.VMEM)
+
+
+def project_kernel(x_ref, gain_ref, left_ref, right_ref, both_ref):
+    seqs = both_ref.shape[1]
+    width = gain_ref.shape[1]
+    local_res = x_ref.shape[1] // width
+    sides = ([], [])
+    for r in range(local_res):
+        values = x_ref[:, r * width : (r + 1) * width].astype(jnp.float32)
+        centred = values - jnp.mean(values, axis=-1, keepdims=True)
+        variance = jnp.mean(centred * centred, axis=-1, keepdims=True)
+        normed = (centred * lax.rsqrt(variance + 1e-05) * gain_ref[...]).astype(jnp.bfloat16)
+        for side, weight_ref in zip(sides, (left_ref, right_ref)):
+            side.append(
+                lax.dot_general(
+                    normed, weight_ref[...], (((1,), (1,)), ((), ())),
+                    preferred_element_type=jnp.float32,
+                )
+            )
+    for n, side in enumerate(sides):
+        both_ref[n] = jnp.concatenate(side, axis=1).astype(jnp.bfloat16)
+
+
+def pair_kernel(pitch, place_ref, left_ref, *refs):
+    *right_refs, weight_ref, bias_ref, out_ref, terms, rows = refs
+    pieces = len(right_refs)
+    local_res, _, features = out_ref.shape
+    lanes = left_ref.shape[1]
+    channels = lanes // local_res
+    per_piece = lanes // channels
+    inv_count = 1.0 / left_ref.shape[0]
+    left_t = left_ref[...].T
+    for n, right_ref in enumerate(right_refs):
+        product = jnp.dot(left_t, right_ref[...], preferred_element_type=jnp.float32)
+        at = place_ref[0] ^ n
+        for i in range(local_res):
+            first = pl.multiple_of((i * pieces + at) * pitch, 8)
+            terms[pl.ds(first, channels), :] = product[i * channels : (i + 1) * channels]
+    count = local_res * pieces
+    outer = jnp.concatenate(
+        [terms[pl.ds(c, count, stride=pitch), :].astype(jnp.bfloat16) for c in range(channels)], axis=1
+    )
+    owner = lax.broadcasted_iota(jnp.int32, outer.shape, 1) % lanes // channels
+    spread = jnp.concatenate(
+        [jnp.where(owner == j, outer, jnp.zeros_like(outer)) for j in range(per_piece)], axis=0
+    )
+    weight = jnp.concatenate(
+        [weight_ref[c * channels : (c + 1) * channels] for c in range(channels) for _ in range(per_piece)], axis=0
+    )
+    total = jnp.dot(spread, weight, preferred_element_type=jnp.float32)
+    total = total * inv_count + bias_ref[...]
+    for j in range(per_piece):
+        rows[pl.ds(j, count, stride=per_piece), :] = total[j * count : (j + 1) * count]
+    out_ref[...] = rows[...].reshape(out_ref.shape).astype(out_ref.dtype)
+
+
+def on_device(alignment, ln_gain, proj_left, proj_right, out_weight, out_bias):
+    seq_shards = lax.axis_size("seq")
+    res_shards = lax.axis_size("res")
+    local_seqs, local_res, width = alignment.shape
+    channels = proj_left.shape[1]
+    lanes = local_res * channels
+    features = out_weight.shape[1]
+    both = pl.pallas_call(
+        project_kernel,
+        out_shape=jax.ShapeDtypeStruct((2, local_seqs, lanes), jnp.bfloat16),
+        in_specs=[VMEM] * 4,
+        out_specs=VMEM,
+    )(alignment.reshape(local_seqs, local_res * width), ln_gain.reshape(1, width), proj_left.T, proj_right.T)
+
+    pieces = res_shards // seq_shards
+    res = lax.axis_index("res")
+    seq = lax.axis_index("seq")
+    axes = ("res", "seq")
+
+    def swap(value, bits, cross):
+        pairs = [
+            (r * seq_shards + q, (r ^ bits) * seq_shards + (q ^ cross))
+            for r in range(res_shards)
+            for q in range(seq_shards)
+        ]
+        return lax.ppermute(value, axes, pairs)
+
+    other = lax.ppermute(both, "seq", [(0, 1), (1, 0)])
+    first = seq == 0
+    full = jnp.concatenate((jnp.where(first, both, other), jnp.where(first, other, both)), axis=1)
+    left, right = full[0], full[1]
+    far = swap(right, pieces, 1)
+    home = res // pieces == seq
+    mine = jnp.where(home, right, far)
+    yours = jnp.where(home, far, right)
+    rights = [mine] + [None] * (pieces - 1)
+    for n in sorted(range(1, pieces), key=lambda n: -bin(n).count("1")):
+        rights[n] = swap(yours, n, 1)
+
+    place = (res % pieces).reshape(1)
+    pitch = channels + 8
+    return pl.pallas_call(
+        functools.partial(pair_kernel, pitch),
+        out_shape=jax.ShapeDtypeStruct((local_res, pieces * local_res, features), jnp.bfloat16),
+        in_specs=[pl.BlockSpec(memory_space=pltpu.SMEM)] + [VMEM] * (pieces + 3),
+        out_specs=VMEM,
+        scratch_shapes=[
+            pltpu.VMEM((local_res * pieces * pitch, lanes), jnp.float32),
+            pltpu.VMEM((local_res * pieces * local_res, features), jnp.float32),
+        ],
+    )(place, left, *rights, out_weight, out_bias.reshape(1, features))
+
+
+def swaps_fit(mesh):
+    res_shards, seq_shards = mesh.shape["res"], mesh.shape["seq"]
+    return seq_shards == 2 and res_shards in (2, 4, 8)
+
+
 def solution(mesh):
     placed = (P(("groups", "seq"), "res", None), P(), P(), P(), P(), P())
     return jax.shard_map(
-        on_device,
+        on_device if swaps_fit(mesh) else gathered,
         mesh=mesh,
         in_specs=placed,
         out_specs=P(("groups", "res"), "seq", None),

time: 45.3 us -> 21 us (0.46)
  blocking collectives: 34.5 us -> 0 us
  waiting for transfers between devices: 0.01 us -> 5.45 us
  starting transfers between devices: 3.29 us -> 7.32 us
  Pallas kernels: 0 us -> 3.96 us
  local copies, waits for them, and re-layouts: 4.41 us -> 2.07 us
  matrix products: 1.15 us -> 0 us
  other arithmetic: 1.34 us -> 1.94 us
    all_gather x2 -> x0, blocking collectives: 34.5 us -> none  [the longest x1 32.6 us: on_device(): right_all = lax.all_gather(right_side, 'res', axis=1, tiled=True)]
    ppermute x0 -> x5, starting transfers between devices: none -> 7.32 us  [the longest x4 6.82 us: swap(): return lax.ppermute(value, axes, pairs)]
    ppermute x0 -> x5, waiting for transfers between devices: none -> 5.45 us  [the longest x4 4.4 us: swap(): return lax.ppermute(value, axes, pairs)]
    pallas_call x0 -> x2, Pallas kernels: none -> 3.96 us  [the longest x1 2.1 us: on_device(): pl.pallas_call(functools.partial(pair_kernel, pitch), out_shape=jax.Shape...]
    all_to_all x1 -> x0, starting transfers between devices: 3.29 us -> none  [on_device(): lax.all_to_all(split_right, 'seq', split_axis=1, concat_axis=0, tiled=True)]
    select_n x0 -> x2, other arithmetic: none -> 1.33 us  [the longest x1 0.72 us: on_device(): jnp.where(first, other, both)]
    reduce_sum x2 -> x0, other arithmetic: 1.19 us -> none  [the longest x1 1.02 us: normalize(): centred = values - jnp.mean(values, axis=-1, keepdims=True)]
    dot_general x3 -> x0, matrix products: 1.15 us -> none  [the longest x1 0.87 us: advance(): jnp.dot(outer_terms, weight_full, precision=lax.Precision.HIGHEST)]
  transfers between devices with their start and end apart: 1 -> 5, of which waited for: 0 -> 5; matrix products, arithmetic and copies ran while one was open for 0% -> 0% of each run, Pallas kernels for 0% -> 0%
where the time goes in v1:
time: 21 us; the launch traced here: 20.7 us
  starting transfers between devices  7.32 us (35%)
  waiting for transfers between devices  5.45 us (26%)
  Pallas kernels  3.96 us (19%)
  local copies, waits for them, and re-layouts  2.07 us (10%)
  other arithmetic  1.94 us (9%)
    ppermute x4, starting transfers between devices, swap(): return lax.ppermute(value, axes, pairs)  6.82 us
    ppermute x4, waiting for transfers between devices, swap(): return lax.ppermute(value, axes, pairs)  4.4 us
    pallas_call x1, Pallas kernels, on_device(): pl.pallas_call(functools.partial(pair_kernel, pitch), out_shape=jax.Shape...  2.1 us
    unnamed x7, local copies, waits for them, and re-layouts  2.07 us
    pallas_call x1, Pallas kernels, on_device(): pl.pallas_call(project_kernel, out_shape=jax.ShapeDtypeStruct((2, local_s...  1.86 us
    ppermute x1, waiting for transfers between devices, on_device(): other = lax.ppermute(both, 'seq', [(0, 1), (1, 0)])  1.05 us
    select_n x1, other arithmetic, on_device(): jnp.where(first, other, both)  0.72 us
    squeeze x1, other arithmetic, on_device(): left, right = (full[0], full[1])  0.61 us
  transfers between devices with their start and end apart: 5, of which 5 were waited for; matrix products, arithmetic and copies ran while one was open for 0% of the time, Pallas kernels for 0%

profile of v1, /device:TPU:0, one launch (start us, length us, event | category | flops | bytes accessed | tf_op | source)
XLA Modules:
  0.0 20.7 jit_solution(12293509545151218284)
XLA Ops:
  0.0 1.5 %copy.7 = bf16[4,8,4,256]{3,1,2,0:T(8,128)(2,1)} copy(bf16[4,8,4,256]{3,2,1,0:T(4,128)(2,1)} %bitcast.12) | data formatting | bytes 131072
  1.5 1.9 %shard_map.64 = bf16[2,32,128]{2,1,0:T(8,128)(2,1)} custom-call(bf16[32,1024]{1,0:T(8,128)(2,1)} %bitcast.11, f32[1,256]{1,0:T(1,128)} %bitcast.15, bf16[32,256]{1,0:T(8,128)(2,1)} %bitcast.13, bf16[32,256]{1,0:T(8,128)(2,1)} %bitcast.14), custom_call_target="tpu_custom_call" | custom-call | tf_op jit(solution)/shard_map/pallas_call | solution.py:136
  3.3 0.5 %collective-permute-start = (bf16[2,32,128]{2,1,0:T(8,128)(2,1)}, bf16[2,32,128]{2,1,0:T(8,128)(2,1)S(1)}, u32[]{:S(2)}, u32[]{:S(2)}) collective-permute-start(bf16[2,32,128]{2,1,0:T(8,128)(2,1)} %shard_map.64), channel_id=1, source_target_pairs={{0,1},{1,0},{2,3},{3,2},{4,5},{5,4},{6,7},{7,6},{8,9},{9,8},{10,11... | collective-permute-start | bytes 49160 | tf_op jit(solution)/shard_map/ppermute | solution.py:156
  3.8 1.0 %collective-permute-done = bf16[2,32,128]{2,1,0:T(8,128)(2,1)S(1)} collective-permute-done((bf16[2,32,128]{2,1,0:T(8,128)(2,1)}, bf16[2,32,128]{2,1,0:T(8,128)(2,1)S(1)}, u32[]{:S(2)}, u32[]{:S(2)}) %collective-permute-start) | collective-permute-done | bytes 16416 | tf_op jit(solution)/shard_map/ppermute | solution.py:156
  4.9 0.7 %broadcast_select_fusion.2 = (bf16[2,32,128]{2,1,0:T(8,128)(2,1)S(1)}, bf16[2,32,128]{2,1,0:T(8,128)(2,1)S(1)}) fusion(bf16[2,32,128]{2,1,0:T(8,128)(2,1)S(1)} %collective-permute-done, bf16[2,32,128]{2,1,0:T(8,128)(2,1)} %shard_map.64, pred[]{:T(512)S(6)} %eq.8), kind=kLoop, calls=%fused_computation.8 | loop fusion | flops 16384 | bytes 65537 | tf_op jit(solution)/shard_map/jit(_where)/select_n | solution.py:158
  5.6 0.6 %fusion.2 = (bf16[64,128]{1,0:T(8,128)(2,1)S(1)}, bf16[64,128]{1,0:T(8,128)(2,1)}) fusion(bf16[2,32,128]{2,1,0:T(8,128)(2,1)S(1)} %get-tuple-element.9, bf16[2,32,128]{2,1,0:T(8,128)(2,1)S(1)} %get-tuple-element.10), kind=kLoop, calls=%fused_computation.5 | loop fusion | flops 65536 | bytes 65536 | tf_op jit(solution)/shard_map/squeeze | solution.py:159
  6.2 3.7 %collective-permute-start.1 = (bf16[64,128]{1,0:T(8,128)(2,1)S(1)}, bf16[64,128]{1,0:T(8,128)(2,1)S(1)}, u32[]{:S(2)}, u32[]{:S(2)}) collective-permute-start(bf16[64,128]{1,0:T(8,128)(2,1)S(1)} %get-tuple-element.7), channel_id=1, source_target_pairs={{0,9},{1,8},{2,11},{3,10},{4,13},{5,12},{6,15},{7,14},{8,1},{9,0},... | collective-permute-start | bytes 49160 | tf_op jit(solution)/shard_map/ppermute | solution.py:154
  9.9 1.4 %collective-permute-done.1 = bf16[64,128]{1,0:T(8,128)(2,1)S(1)} collective-permute-done((bf16[64,128]{1,0:T(8,128)(2,1)S(1)}, bf16[64,128]{1,0:T(8,128)(2,1)S(1)}, u32[]{:S(2)}, u32[]{:S(2)}) %collective-permute-start.1) | collective-permute-done | bytes 16416 | tf_op jit(solution)/shard_map/ppermute | solution.py:154
  11.3 0.6 %broadcast_select_fusion = (bf16[64,128]{1,0:T(8,128)(2,1)S(1)}, bf16[64,128]{1,0:T(8,128)(2,1)}) fusion(bf16[64,128]{1,0:T(8,128)(2,1)S(1)} %collective-permute-done.1, bf16[64,128]{1,0:T(8,128)(2,1)S(1)} %get-tuple-element.7, pred[]{:T(512)S(6)} %eq.9), kind=kLoop, calls=%fused_computation.6 | loop fusion | flops 16384 | bytes 65537 | tf_op jit(solution)/shard_map/jit(_where)/select_n | solution.py:163
  12.0 2.5 %collective-permute-start.4 = (bf16[64,128]{1,0:T(8,128)(2,1)S(1)}, bf16[64,128]{1,0:T(8,128)(2,1)S(1)}, u32[]{:S(2)}, u32[]{:S(2)}) collective-permute-start(bf16[64,128]{1,0:T(8,128)(2,1)S(1)} %get-tuple-element.5), channel_id=1, source_target_pairs={{0,7},{1,6},{2,5},{3,4},{4,3},{5,2},{6,1},{7,0},{8,15},{9,14},{10,... | collective-permute-start | bytes 49160 | tf_op jit(solution)/shard_map/ppermute | solution.py:154
  14.5 0.4 %collective-permute-start.3 = (bf16[64,128]{1,0:T(8,128)(2,1)S(1)}, bf16[64,128]{1,0:T(8,128)(2,1)S(1)}, u32[]{:S(2)}, u32[]{:S(2)}) collective-permute-start(bf16[64,128]{1,0:T(8,128)(2,1)S(1)} %get-tuple-element.5), channel_id=1, source_target_pairs={{0,5},{1,4},{2,7},{3,6},{4,1},{5,0},{6,3},{7,2},{8,13},{9,12},{10,... | collective-permute-start | bytes 49160 | tf_op jit(solution)/shard_map/ppermute | solution.py:154
  14.9 0.2 collective-permute-start.2
  15.1 0.9 %collective-permute-done.4.refs_3_ = bf16[64,128]{1,0:T(8,128)(2,1)S(1)} collective-permute-done((bf16[64,128]{1,0:T(8,128)(2,1)S(1)}, bf16[64,128]{1,0:T(8,128)(2,1)S(1)}, u32[]{:S(2)}, u32[]{:S(2)}) %collective-permute-start.4) | collective-permute-done | bytes 16416 | tf_op jit(solution)/shard_map/ppermute | solution.py:154
  16.0 0.0 copy-start
  16.0 1.6 %collective-permute-done.3.refs_2_ = bf16[64,128]{1,0:T(8,128)(2,1)S(1)} collective-permute-done((bf16[64,128]{1,0:T(8,128)(2,1)S(1)}, bf16[64,128]{1,0:T(8,128)(2,1)S(1)}, u32[]{:S(2)}, u32[]{:S(2)}) %collective-permute-start.3) | collective-permute-done | bytes 16416 | tf_op jit(solution)/shard_map/ppermute | solution.py:154
  17.7 0.0 copy-start.1
  17.7 0.4 %collective-permute-done.2.refs_1_ = bf16[64,128]{1,0:T(8,128)(2,1)S(1)} collective-permute-done((bf16[64,128]{1,0:T(8,128)(2,1)S(1)}, bf16[64,128]{1,0:T(8,128)(2,1)S(1)}, u32[]{:S(2)}, u32[]{:S(2)}) %collective-permute-start.2) | collective-permute-done | bytes 16416 | tf_op jit(solution)/shard_map/ppermute | solution.py:154
  18.1 0.0 copy-start.2
  18.1 0.0 copy-done
  18.1 0.2 copy-done.1
  18.3 0.4 %copy-done.2 = bf16[64,128]{1,0:T(8,128)(2,1)} copy-done((bf16[64,128]{1,0:T(8,128)(2,1)}, bf16[64,128]{1,0:T(8,128)(2,1)S(1)}, u32[]{:S(2)}) %copy-start.2) | copy-done | bytes 16408
  18.7 2.1 %shard_map.65 = bf16[4,16,128]{2,1,0:T(8,128)(2,1)} custom-call(s32[1]{0:T(128)} %bitcast.place_ref, bf16[64,128]{1,0:T(8,128)(2,1)} %get-tuple-element.8.left_ref, bf16[64,128]{1,0:T(8,128)(2,1)} %get-tuple-element.6.refs_0_, bf16[64,128]{1,0:T(8,128)(2,1)} %copy-done.2, bf16[64,128]{1,0:T(8,128)(2,1)} %copy-done.1, bf16[64,128]{1,0:T(8,128)(2,1)} %copy-done, ...), custom_call_target="tpu_custom_call" | custom-call | tf_op jit(solution)/shard_map/pallas_call | solution.py:170
Async XLA Ops:
  3.3 1.5 %collective-permute-start = (bf16[2,32,128]{2,1,0:T(8,128)(2,1)}, bf16[2,32,128]{2,1,0:T(8,128)(2,1)S(1)}, u32[]{:S(2)}, u32[]{:S(2)}) collective-permute-start(bf16[2,32,128]{2,1,0:T(8,128)(2,1)} %shard_map.64), channel_id=1, source_target_pairs={{0,1},{1,0},{2,3},{3,2},{4,5},{5,4},{6,7},{7,6},{8,9},{9,8},{10,11... | collective-permute-start | bytes 49160 | tf_op jit(solution)/shard_map/ppermute | solution.py:156
  6.2 5.1 %collective-permute-start.1 = (bf16[64,128]{1,0:T(8,128)(2,1)S(1)}, bf16[64,128]{1,0:T(8,128)(2,1)S(1)}, u32[]{:S(2)}, u32[]{:S(2)}) collective-permute-start(bf16[64,128]{1,0:T(8,128)(2,1)S(1)} %get-tuple-element.7), channel_id=1, source_target_pairs={{0,9},{1,8},{2,11},{3,10},{4,13},{5,12},{6,15},{7,14},{8,1},{9,0},... | collective-permute-start | bytes 49160 | tf_op jit(solution)/shard_map/ppermute | solution.py:154
  12.0 4.1 %collective-permute-start.4 = (bf16[64,128]{1,0:T(8,128)(2,1)S(1)}, bf16[64,128]{1,0:T(8,128)(2,1)S(1)}, u32[]{:S(2)}, u32[]{:S(2)}) collective-permute-start(bf16[64,128]{1,0:T(8,128)(2,1)S(1)} %get-tuple-element.5), channel_id=1, source_target_pairs={{0,7},{1,6},{2,5},{3,4},{4,3},{5,2},{6,1},{7,0},{8,15},{9,14},{10,... | collective-permute-start | bytes 49160 | tf_op jit(solution)/shard_map/ppermute | solution.py:154
  14.5 3.2 %collective-permute-start.3 = (bf16[64,128]{1,0:T(8,128)(2,1)S(1)}, bf16[64,128]{1,0:T(8,128)(2,1)S(1)}, u32[]{:S(2)}, u32[]{:S(2)}) collective-permute-start(bf16[64,128]{1,0:T(8,128)(2,1)S(1)} %get-tuple-element.5), channel_id=1, source_target_pairs={{0,5},{1,4},{2,7},{3,6},{4,1},{5,0},{6,3},{7,2},{8,13},{9,12},{10,... | collective-permute-start | bytes 49160 | tf_op jit(solution)/shard_map/ppermute | solution.py:154
  14.9 3.2 %collective-permute-start.2 = (bf16[64,128]{1,0:T(8,128)(2,1)S(1)}, bf16[64,128]{1,0:T(8,128)(2,1)S(1)}, u32[]{:S(2)}, u32[]{:S(2)}) collective-permute-start(bf16[64,128]{1,0:T(8,128)(2,1)S(1)} %get-tuple-element.5), channel_id=1, source_target_pairs={{0,3},{1,2},{2,1},{3,0},{4,7},{5,6},{6,5},{7,4},{8,11},{9,10},{10,... | collective-permute-start | bytes 49160 | tf_op jit(solution)/shard_map/ppermute | solution.py:154
  16.0 2.0 %copy-start = (bf16[64,128]{1,0:T(8,128)(2,1)}, bf16[64,128]{1,0:T(8,128)(2,1)S(1)}, u32[]{:S(2)}) copy-start(bf16[64,128]{1,0:T(8,128)(2,1)S(1)} %collective-permute-done.4.refs_3_) | copy-start | bytes 49156
  17.7 0.6 %copy-start.1 = (bf16[64,128]{1,0:T(8,128)(2,1)}, bf16[64,128]{1,0:T(8,128)(2,1)S(1)}, u32[]{:S(2)}) copy-start(bf16[64,128]{1,0:T(8,128)(2,1)S(1)} %collective-permute-done.3.refs_2_) | copy-start | bytes 49156
  18.1 0.6 %copy-start.2 = (bf16[64,128]{1,0:T(8,128)(2,1)}, bf16[64,128]{1,0:T(8,128)(2,1)S(1)}, u32[]{:S(2)}) copy-start(bf16[64,128]{1,0:T(8,128)(2,1)S(1)} %collective-permute-done.2.refs_1_) | copy-start | bytes 49156

commit v2 on v1

--- a/solution.py
+++ b/solution.py
@@ -70,15 +70,34 @@
 
 
 VMEM = pl.BlockSpec(memory_space=pltpu.VMEM)
-
-
-def project_kernel(x_ref, gain_ref, left_ref, right_ref, both_ref):
-    seqs = both_ref.shape[1]
-    width = gain_ref.shape[1]
-    local_res = x_ref.shape[1] // width
+HBM = pl.BlockSpec(memory_space=pltpu.HBM)
+
+
+def near(value):
+    return pltpu.with_memory_space_constraint(value, pltpu.VMEM)
+
+
+def project_kernel(x_hbm, gain_hbm, left_hbm, right_hbm, both_ref, x_ref, gain_ref, left_ref, right_ref, rows, sems):
+    copies = [
+        pltpu.make_async_copy(source, target, sems.at[n])
+        for n, (source, target) in enumerate(
+            ((x_hbm, x_ref), (gain_hbm, gain_ref), (left_hbm, left_ref), (right_hbm, right_ref))
+        )
+    ]
+    for copy in copies:
+        copy.start()
+    for copy in copies:
+        copy.wait()
+    seqs, local_res, width = x_ref.shape
+    tiles, _, lanes = rows.shape
+    for n in range(tiles):
+        part = x_ref[:, :, n * lanes : (n + 1) * lanes].astype(jnp.float32)
+        rows[n] = part.reshape(seqs * local_res, lanes)
     sides = ([], [])
     for r in range(local_res):
-        values = x_ref[:, r * width : (r + 1) * width].astype(jnp.float32)
+        values = jnp.concatenate(
+            [rows[n, pl.ds(r, seqs, stride=local_res), :] for n in range(tiles)], axis=1
+        )
         centred = values - jnp.mean(values, axis=-1, keepdims=True)
         variance = jnp.mean(centred * centred, axis=-1, keepdims=True)
         normed = (centred * lax.rsqrt(variance + 1e-05) * gain_ref[...]).astype(jnp.bfloat16)
@@ -94,7 +113,9 @@
 
 
 def pair_kernel(pitch, place_ref, left_ref, *refs):
-    *right_refs, weight_ref, bias_ref, out_ref, terms, rows = refs
+    *right_refs, weight_ref, bias_hbm, out_ref, terms, rows, bias_ref, sem = refs
+    bias_copy = pltpu.make_async_copy(bias_hbm, bias_ref, sem)
+    bias_copy.start()
     pieces = len(right_refs)
     local_res, _, features = out_ref.shape
     lanes = left_ref.shape[1]
@@ -120,6 +141,7 @@
         [weight_ref[c * channels : (c + 1) * channels] for c in range(channels) for _ in range(per_piece)], axis=0
     )
     total = jnp.dot(spread, weight, preferred_element_type=jnp.float32)
+    bias_copy.wait()
     total = total * inv_count + bias_ref[...]
     for j in range(per_piece):
         rows[pl.ds(j, count, stride=per_piece), :] = total[j * count : (j + 1) * count]
@@ -135,10 +157,18 @@
     features = out_weight.shape[1]
     both = pl.pallas_call(
         project_kernel,
-        out_shape=jax.ShapeDtypeStruct((2, local_seqs, lanes), jnp.bfloat16),
-        in_specs=[VMEM] * 4,
+        out_shape=pltpu.VMEM((2, local_seqs, lanes), jnp.bfloat16),
+        in_specs=[HBM] * 4,
         out_specs=VMEM,
-    )(alignment.reshape(local_seqs, local_res * width), ln_gain.reshape(1, width), proj_left.T, proj_right.T)
+        scratch_shapes=[
+            pltpu.VMEM(alignment.shape, alignment.dtype),
+            pltpu.VMEM((1, width), jnp.float32),
+            pltpu.VMEM((channels, width), proj_left.dtype),
+            pltpu.VMEM((channels, width), proj_right.dtype),
+            pltpu.VMEM((width // 128, local_seqs * local_res, 128), jnp.float32),
+            pltpu.SemaphoreType.DMA((4,)),
+        ],
+    )(alignment, ln_gain.reshape(1, width), proj_left.T, proj_right.T)
 
     pieces = res_shards // seq_shards
     res = lax.axis_index("res")
@@ -170,13 +200,15 @@
     return pl.pallas_call(
         functools.partial(pair_kernel, pitch),
         out_shape=jax.ShapeDtypeStruct((local_res, pieces * local_res, features), jnp.bfloat16),
-        in_specs=[pl.BlockSpec(memory_space=pltpu.SMEM)] + [VMEM] * (pieces + 3),
+        in_specs=[pl.BlockSpec(memory_space=pltpu.SMEM)] + [VMEM] * (pieces + 2) + [HBM],
         out_specs=VMEM,
         scratch_shapes=[
             pltpu.VMEM((local_res * pieces * pitch, lanes), jnp.float32),
             pltpu.VMEM((local_res * pieces * local_res, features), jnp.float32),
+            pltpu.VMEM((1, features), jnp.float32),
+            pltpu.SemaphoreType.DMA(()),
         ],
-    )(place, left, *rights, out_weight, out_bias.reshape(1, features))
+    )(place, *(near(v) for v in (left, *rights, out_weight)), out_bias.reshape(1, features))
 
 
 def swaps_fit(mesh):

time: 21 us -> 15.9 us (0.76)
  local copies, waits for them, and re-layouts: 2.07 us -> 0.01 us
  other arithmetic: 1.94 us -> 0.02 us
  Pallas kernels: 3.96 us -> 2.97 us
    unnamed x7 -> x2, local copies, waits for them, and re-layouts: 2.07 us -> 0.01 us
    select_n x1, other arithmetic: 0.72 us -> 0.01 us  [on_device(): jnp.where(first, other, both)]
    squeeze x1, other arithmetic: 0.61 us -> 0.01 us  [on_device(): left, right = (full[0], full[1])]
    select_n x1, other arithmetic: 0.61 us -> 0.01 us  [on_device(): yours = jnp.where(home, far, right)]
    pallas_call x1, Pallas kernels: 1.86 us -> 1.34 us  [on_device(): pl.pallas_call(project_kernel, out_shape=pltpu.VMEM((2, local_seqs, lanes...]
    pallas_call x1, Pallas kernels: 2.1 us -> 1.63 us  [on_device(): pl.pallas_call(functools.partial(pair_kernel, pitch), out_shape=jax.Shape...]
    ppermute x1, waiting for transfers between devices: 1.05 us -> 0.84 us  [on_device(): other = lax.ppermute(both, 'seq', [(0, 1), (1, 0)])]
where the time goes in v2:
time: 15.9 us; the launch traced here: 15.7 us
  starting transfers between devices  7.45 us (47%)
  waiting for transfers between devices  5.24 us (33%)
  Pallas kernels  2.97 us (19%)
    ppermute x4, starting transfers between devices, swap(): return lax.ppermute(value, axes, pairs)  6.89 us
    ppermute x4, waiting for transfers between devices, swap(): return lax.ppermute(value, axes, pairs)  4.4 us
    pallas_call x1, Pallas kernels, on_device(): pl.pallas_call(functools.partial(pair_kernel, pitch), out_shape=jax.Shape...  1.63 us
    pallas_call x1, Pallas kernels, on_device(): pl.pallas_call(project_kernel, out_shape=pltpu.VMEM((2, local_seqs, lanes...  1.34 us
    ppermute x1, waiting for transfers between devices, on_device(): other = lax.ppermute(both, 'seq', [(0, 1), (1, 0)])  0.84 us
    ppermute x1, starting transfers between devices, on_device(): other = lax.ppermute(both, 'seq', [(0, 1), (1, 0)])  0.56 us
  transfers between devices with their start and end apart: 5, of which 5 were waited for; matrix products, arithmetic and copies ran while one was open for 0% of the time, Pallas kernels for 0%

profile of v2, /device:TPU:0, one launch (start us, length us, event | category | flops | bytes accessed | tf_op | source)
XLA Modules:
  0.0 15.7 jit_solution(13636535505955127631)
XLA Ops:
  0.0 0.0 copy-start
  0.0 1.3 %shard_map.64 = bf16[2,32,128]{2,1,0:T(8,128)(2,1)S(1)} custom-call(bf16[32,4,256]{2,1,0:T(4,128)(2,1)} %x_hbm.1, f32[1,256]{1,0:T(1,128)} %bitcast.11, bf16[32,256]{1,0:T(8,128)(2,1)} %bitcast.9, bf16[32,256]{1,0:T(8,128)(2,1)} %bitcast.10), custom_call_target="tpu_custom_call" | custom-call | tf_op jit(solution)/shard_map/pallas_call | solution.py:158
  1.3 0.6 %collective-permute-start = (bf16[2,32,128]{2,1,0:T(8,128)(2,1)S(1)}, bf16[2,32,128]{2,1,0:T(8,128)(2,1)S(1)}, u32[]{:S(2)}, u32[]{:S(2)}) collective-permute-start(bf16[2,32,128]{2,1,0:T(8,128)(2,1)S(1)} %shard_map.64), channel_id=1, source_target_pairs={{0,1},{1,0},{2,3},{3,2},{4,5},{5,4},{6,7},{7,6},{8,9},{9,8},{10,11... | collective-permute-start | bytes 49160 | tf_op jit(solution)/shard_map/ppermute | solution.py:186
  1.9 0.8 %collective-permute-done = bf16[2,32,128]{2,1,0:T(8,128)(2,1)S(1)} collective-permute-done((bf16[2,32,128]{2,1,0:T(8,128)(2,1)S(1)}, bf16[2,32,128]{2,1,0:T(8,128)(2,1)S(1)}, u32[]{:S(2)}, u32[]{:S(2)}) %collective-permute-start) | collective-permute-done | bytes 16416 | tf_op jit(solution)/shard_map/ppermute | solution.py:186
  2.8 3.8 %collective-permute-start.1 = (bf16[64,128]{1,0:T(8,128)(2,1)S(1)}, bf16[64,128]{1,0:T(8,128)(2,1)S(1)}, u32[]{:S(2)}, u32[]{:S(2)}) collective-permute-start(bf16[64,128]{1,0:T(8,128)(2,1)S(1)} %get-tuple-element.7), channel_id=1, source_target_pairs={{0,9},{1,8},{2,11},{3,10},{4,13},{5,12},{6,15},{7,14},{8,1},{9,0},... | collective-permute-start | bytes 49160 | tf_op jit(solution)/shard_map/ppermute | solution.py:184
  6.5 1.4 %collective-permute-done.1 = bf16[64,128]{1,0:T(8,128)(2,1)S(1)} collective-permute-done((bf16[64,128]{1,0:T(8,128)(2,1)S(1)}, bf16[64,128]{1,0:T(8,128)(2,1)S(1)}, u32[]{:S(2)}, u32[]{:S(2)}) %collective-permute-start.1) | collective-permute-done | bytes 16416 | tf_op jit(solution)/shard_map/ppermute | solution.py:184
  8.0 2.5 %collective-permute-start.4 = (bf16[64,128]{1,0:T(8,128)(2,1)S(1)}, bf16[64,128]{1,0:T(8,128)(2,1)S(1)}, u32[]{:S(2)}, u32[]{:S(2)}) collective-permute-start(bf16[64,128]{1,0:T(8,128)(2,1)S(1)} %get-tuple-element.5), channel_id=1, source_target_pairs={{0,7},{1,6},{2,5},{3,4},{4,3},{5,2},{6,1},{7,0},{8,15},{9,14},{10,... | collective-permute-start | bytes 49160 | tf_op jit(solution)/shard_map/ppermute | solution.py:184
  10.5 0.4 %collective-permute-start.3 = (bf16[64,128]{1,0:T(8,128)(2,1)S(1)}, bf16[64,128]{1,0:T(8,128)(2,1)S(1)}, u32[]{:S(2)}, u32[]{:S(2)}) collective-permute-start(bf16[64,128]{1,0:T(8,128)(2,1)S(1)} %get-tuple-element.5), channel_id=1, source_target_pairs={{0,5},{1,4},{2,7},{3,6},{4,1},{5,0},{6,3},{7,2},{8,13},{9,12},{10,... | collective-permute-start | bytes 49160 | tf_op jit(solution)/shard_map/ppermute | solution.py:184
  10.9 0.2 %collective-permute-start.2 = (bf16[64,128]{1,0:T(8,128)(2,1)S(1)}, bf16[64,128]{1,0:T(8,128)(2,1)S(1)}, u32[]{:S(2)}, u32[]{:S(2)}) collective-permute-start(bf16[64,128]{1,0:T(8,128)(2,1)S(1)} %get-tuple-element.5), channel_id=1, source_target_pairs={{0,3},{1,2},{2,1},{3,0},{4,7},{5,6},{6,5},{7,4},{8,11},{9,10},{10,... | collective-permute-start | bytes 49160 | tf_op jit(solution)/shard_map/ppermute | solution.py:184
  11.1 0.9 %collective-permute-done.4.refs_3_ = bf16[64,128]{1,0:T(8,128)(2,1)S(1)} collective-permute-done((bf16[64,128]{1,0:T(8,128)(2,1)S(1)}, bf16[64,128]{1,0:T(8,128)(2,1)S(1)}, u32[]{:S(2)}, u32[]{:S(2)}) %collective-permute-start.4) | collective-permute-done | bytes 16416 | tf_op jit(solution)/shard_map/ppermute | solution.py:184
  12.0 1.6 %collective-permute-done.3.refs_2_ = bf16[64,128]{1,0:T(8,128)(2,1)S(1)} collective-permute-done((bf16[64,128]{1,0:T(8,128)(2,1)S(1)}, bf16[64,128]{1,0:T(8,128)(2,1)S(1)}, u32[]{:S(2)}, u32[]{:S(2)}) %collective-permute-start.3) | collective-permute-done | bytes 16416 | tf_op jit(solution)/shard_map/ppermute | solution.py:184
  13.7 0.4 %collective-permute-done.2.refs_1_ = bf16[64,128]{1,0:T(8,128)(2,1)S(1)} collective-permute-done((bf16[64,128]{1,0:T(8,128)(2,1)S(1)}, bf16[64,128]{1,0:T(8,128)(2,1)S(1)}, u32[]{:S(2)}, u32[]{:S(2)}) %collective-permute-start.2) | collective-permute-done | bytes 16416 | tf_op jit(solution)/shard_map/ppermute | solution.py:184
  14.1 0.0 copy-done
  14.1 1.6 %shard_map.65 = bf16[4,16,128]{2,1,0:T(8,128)(2,1)} custom-call(s32[1]{0:T(128)} %bitcast.place_ref, bf16[64,128]{1,0:T(8,128)(2,1)S(1)} %get-tuple-element.8.left_ref, bf16[64,128]{1,0:T(8,128)(2,1)S(1)} %get-tuple-element.6.refs_0_, bf16[64,128]{1,0:T(8,128)(2,1)S(1)} %collective-permute-done.2.refs_1_, ...), custom_call_target="tpu_custom_call" | custom-call | tf_op jit(solution)/shard_map/pallas_call | solution.py:200
  (3 shorter events, 0.0 us)
Async XLA Ops:
  0.0 14.1 %copy-start = (bf16[1024,128]{1,0:T(8,128)(2,1)S(1)}, bf16[1024,128]{1,0:T(8,128)(2,1)}, u32[]{:S(2)}) copy-start(bf16[1024,128]{1,0:T(8,128)(2,1)} %refs_4_.1) | copy-start | bytes 786436
  1.3 1.4 %collective-permute-start = (bf16[2,32,128]{2,1,0:T(8,128)(2,1)S(1)}, bf16[2,32,128]{2,1,0:T(8,128)(2,1)S(1)}, u32[]{:S(2)}, u32[]{:S(2)}) collective-permute-start(bf16[2,32,128]{2,1,0:T(8,128)(2,1)S(1)} %shard_map.64), channel_id=1, source_target_pairs={{0,1},{1,0},{2,3},{3,2},{4,5},{5,4},{6,7},{7,6},{8,9},{9,8},{10,11... | collective-permute-start | bytes 49160 | tf_op jit(solution)/shard_map/ppermute | solution.py:186
  2.8 5.2 %collective-permute-start.1 = (bf16[64,128]{1,0:T(8,128)(2,1)S(1)}, bf16[64,128]{1,0:T(8,128)(2,1)S(1)}, u32[]{:S(2)}, u32[]{:S(2)}) collective-permute-start(bf16[64,128]{1,0:T(8,128)(2,1)S(1)} %get-tuple-element.7), channel_id=1, source_target_pairs={{0,9},{1,8},{2,11},{3,10},{4,13},{5,12},{6,15},{7,14},{8,1},{9,0},... | collective-permute-start | bytes 49160 | tf_op jit(solution)/shard_map/ppermute | solution.py:184
  8.0 4.1 %collective-permute-start.4 = (bf16[64,128]{1,0:T(8,128)(2,1)S(1)}, bf16[64,128]{1,0:T(8,128)(2,1)S(1)}, u32[]{:S(2)}, u32[]{:S(2)}) collective-permute-start(bf16[64,128]{1,0:T(8,128)(2,1)S(1)} %get-tuple-element.5), channel_id=1, source_target_pairs={{0,7},{1,6},{2,5},{3,4},{4,3},{5,2},{6,1},{7,0},{8,15},{9,14},{10,... | collective-permute-start | bytes 49160 | tf_op jit(solution)/shard_map/ppermute | solution.py:184
  10.5 3.2 %collective-permute-start.3 = (bf16[64,128]{1,0:T(8,128)(2,1)S(1)}, bf16[64,128]{1,0:T(8,128)(2,1)S(1)}, u32[]{:S(2)}, u32[]{:S(2)}) collective-permute-start(bf16[64,128]{1,0:T(8,128)(2,1)S(1)} %get-tuple-element.5), channel_id=1, source_target_pairs={{0,5},{1,4},{2,7},{3,6},{4,1},{5,0},{6,3},{7,2},{8,13},{9,12},{10,... | collective-permute-start | bytes 49160 | tf_op jit(solution)/shard_map/ppermute | solution.py:184
  10.9 3.2 %collective-permute-start.2 = (bf16[64,128]{1,0:T(8,128)(2,1)S(1)}, bf16[64,128]{1,0:T(8,128)(2,1)S(1)}, u32[]{:S(2)}, u32[]{:S(2)}) collective-permute-start(bf16[64,128]{1,0:T(8,128)(2,1)S(1)} %get-tuple-element.5), channel_id=1, source_target_pairs={{0,3},{1,2},{2,1},{3,0},{4,7},{5,6},{6,5},{7,4},{8,11},{9,10},{10,... | collective-permute-start | bytes 49160 | tf_op jit(solution)/shard_map/ppermute | solution.py:184

commit v3 on v2

--- a/solution.py
+++ b/solution.py
@@ -7,6 +7,7 @@
 from jax.experimental import pallas as pl
 from jax.experimental.pallas import tpu as pltpu
 from jax.sharding import PartitionSpec as P
+
 
 def normalize(alignment, ln_gain):
     values = alignment.astype(jnp.float32)
@@ -86,13 +87,14 @@
     ]
     for copy in copies:
         copy.start()
-    for copy in copies:
-        copy.wait()
-    seqs, local_res, width = x_ref.shape
+    copies[0].wait()
+    seqs, local_res, _ = x_ref.shape
     tiles, _, lanes = rows.shape
     for n in range(tiles):
         part = x_ref[:, :, n * lanes : (n + 1) * lanes].astype(jnp.float32)
         rows[n] = part.reshape(seqs * local_res, lanes)
+    for copy in copies[1:]:
+        copy.wait()
     sides = ([], [])
     for r in range(local_res):
         values = jnp.concatenate(
@@ -112,40 +114,58 @@
         both_ref[n] = jnp.concatenate(side, axis=1).astype(jnp.bfloat16)
 
 
-def pair_kernel(pitch, place_ref, left_ref, *refs):
-    *right_refs, weight_ref, bias_hbm, out_ref, terms, rows, bias_ref, sem = refs
+def pair_rows(left_t, pieces, places, local_res, weight_ref, terms, totals, rows):
+    count = local_res * len(pieces)
+    channels = left_t.shape[0] // local_res
+    lanes = pieces[0].shape[1]
+    per_piece = lanes // channels
+    pitch = terms.shape[0] // count
+    for n, piece in enumerate(pieces):
+        product = jnp.dot(left_t, piece, preferred_element_type=jnp.float32)
+        for i in range(local_res):
+            first = (i * len(pieces) + n) * pitch
+            terms[first : first + channels, :] = product[i * channels : (i + 1) * channels]
+    owner = lax.broadcasted_iota(jnp.int32, (count, lanes), 1) // channels
+    spread = []
+    for c in range(channels):
+        term = terms[pl.ds(c, count, stride=pitch), :]
+        parts = [jnp.where(owner == j, term, 0.0) for j in range(per_piece)]
+        spread.append(jnp.concatenate(parts, axis=0).astype(jnp.bfloat16))
+    weight = jnp.concatenate(
+        [weight_ref[c * channels : (c + 1) * channels] for c in range(channels) for _ in range(per_piece)], axis=0
+    )
+    totals[...] = jnp.dot(jnp.concatenate(spread, axis=1), weight, preferred_element_type=jnp.float32)
+    columns = rows.shape[0] // local_res
+    for n, at in enumerate(places):
+        for j in range(per_piece):
+            row = totals[pl.ds(j * count + n, local_res, stride=len(pieces)), :]
+            rows[pl.ds(at * per_piece + j, local_res, stride=columns), :] = row
+
+
+def early_kernel(
+    local_res, slots, place_ref, left_ref, right_ref, weight_ref, bias_hbm, left_t_ref, rows, bias_ref, terms, totals, sem
+):
     bias_copy = pltpu.make_async_copy(bias_hbm, bias_ref, sem)
     bias_copy.start()
-    pieces = len(right_refs)
-    local_res, _, features = out_ref.shape
-    lanes = left_ref.shape[1]
-    channels = lanes // local_res
-    per_piece = lanes // channels
-    inv_count = 1.0 / left_ref.shape[0]
-    left_t = left_ref[...].T
-    for n, right_ref in enumerate(right_refs):
-        product = jnp.dot(left_t, right_ref[...], preferred_element_type=jnp.float32)
-        at = place_ref[0] ^ n
-        for i in range(local_res):
-            first = pl.multiple_of((i * pieces + at) * pitch, 8)
-            terms[pl.ds(first, channels), :] = product[i * channels : (i + 1) * channels]
-    count = local_res * pieces
-    outer = jnp.concatenate(
-        [terms[pl.ds(c, count, stride=pitch), :].astype(jnp.bfloat16) for c in range(channels)], axis=1
-    )
-    owner = lax.broadcasted_iota(jnp.int32, outer.shape, 1) % lanes // channels
-    spread = jnp.concatenate(
-        [jnp.where(owner == j, outer, jnp.zeros_like(outer)) for j in range(per_piece)], axis=0
-    )
-    weight = jnp.concatenate(
-        [weight_ref[c * channels : (c + 1) * channels] for c in range(channels) for _ in range(per_piece)], axis=0
-    )
-    total = jnp.dot(spread, weight, preferred_element_type=jnp.float32)
+    left_t_ref[...] = left_ref[...].T
+    seqs = left_ref.shape[0]
+    pieces = [right_ref[n * seqs : (n + 1) * seqs] for n in range(len(slots))]
+    places = [place_ref[0] ^ slot for slot in slots]
+    rows[...] = jnp.zeros_like(rows)
+    pair_rows(left_t_ref[...], pieces, places, local_res, weight_ref, terms, totals, rows)
     bias_copy.wait()
-    total = total * inv_count + bias_ref[...]
-    for j in range(per_piece):
-        rows[pl.ds(j, count, stride=per_piece), :] = total[j * count : (j + 1) * count]
-    out_ref[...] = rows[...].reshape(out_ref.shape).astype(out_ref.dtype)
+
+
+def late_kernel(
+    slots, place_ref, left_t_ref, early_ref, right_ref, weight_ref, bias_ref, out_ref, rows, terms, totals
+):
+    rows[...] = early_ref[...]
+    seqs = left_t_ref.shape[1]
+    pieces = [right_ref[n * seqs : (n + 1) * seqs] for n in range(len(slots))]
+    places = [place_ref[0] ^ slot for slot in slots]
+    pair_rows(left_t_ref[...], pieces, places, out_ref.shape[0], weight_ref, terms, totals, rows)
+    total = rows[...] * (1.0 / seqs) + bias_ref[...]
+    out_ref[...] = total.reshape(out_ref.shape).astype(out_ref.dtype)
 
 
 def on_device(alignment, ln_gain, proj_left, proj_right, out_weight, out_bias):
@@ -173,47 +193,70 @@
     pieces = res_shards // seq_shards
     res = lax.axis_index("res")
     seq = lax.axis_index("seq")
-    axes = ("res", "seq")
-
-    def swap(value, bits, cross):
-        pairs = [
-            (r * seq_shards + q, (r ^ bits) * seq_shards + (q ^ cross))
-            for r in range(res_shards)
-            for q in range(seq_shards)
-        ]
-        return lax.ppermute(value, axes, pairs)
+    half = res_shards // 2
+
+    def send(value, target):
+        pairs = []
+        for r in range(res_shards):
+            for q in range(seq_shards):
+                to_res, to_seq = target(r, q)
+                pairs.append((r * seq_shards + q, to_res * seq_shards + to_seq))
+        return lax.ppermute(value, ("res", "seq"), pairs)
+
+    def flow(far, near_by):
+        def target(r, q):
+            if q == 0:
+                return r ^ half ^ far, int(r >= half)
+            return (r ^ 1, 1) if r >= half else (r ^ near_by, 0)
+
+        return target
 
     other = lax.ppermute(both, "seq", [(0, 1), (1, 0)])
     first = seq == 0
     full = jnp.concatenate((jnp.where(first, both, other), jnp.where(first, other, both)), axis=1)
     left, right = full[0], full[1]
-    far = swap(right, pieces, 1)
-    home = res // pieces == seq
-    mine = jnp.where(home, right, far)
-    yours = jnp.where(home, far, right)
-    rights = [mine] + [None] * (pieces - 1)
-    for n in sorted(range(1, pieces), key=lambda n: -bin(n).count("1")):
-        rights[n] = swap(yours, n, 1)
-
-    place = (res % pieces).reshape(1)
+    home = res // half == seq
+    one = send(right, flow(0, 1))
+    two = send(right, flow(1, 0))
+    mine = jnp.concatenate((jnp.where(home, right, one), jnp.where(home, one, two)), 0)
+    late = send(mine, lambda r, q: (r ^ 2, q))
+    slots = (0, 1, 2, 3)
+    nseq = right.shape[0]
+    place = (res % half).reshape(1)
+    weight = near(out_weight)
+    columns = pieces * local_res
     pitch = channels + 8
+    count = local_res * 2
+    smem = pl.BlockSpec(memory_space=pltpu.SMEM)
+    scratch = [
+        pltpu.VMEM((count * pitch, lanes), jnp.float32),
+        pltpu.VMEM((count * local_res, features), jnp.float32),
+    ]
+    left_t, early, bias = pl.pallas_call(
+        functools.partial(early_kernel, local_res, slots[:2]),
+        out_shape=[
+            pltpu.VMEM((lanes, nseq), jnp.bfloat16),
+            pltpu.VMEM((local_res * columns, features), jnp.float32),
+            pltpu.VMEM((1, features), jnp.float32),
+        ],
+        in_specs=[smem] + [VMEM] * 3 + [HBM],
+        out_specs=[VMEM] * 3,
+        scratch_shapes=scratch + [pltpu.SemaphoreType.DMA(())],
+        cost_estimate=pl.CostEstimate(flops=10**9, transcendentals=0, bytes_accessed=0),
+        name="early",
+    )(place, near(left), near(mine), weight, out_bias.reshape(1, features))
     return pl.pallas_call(
-        functools.partial(pair_kernel, pitch),
-        out_shape=jax.ShapeDtypeStruct((local_res, pieces * local_res, features), jnp.bfloat16),
-        in_specs=[pl.BlockSpec(memory_space=pltpu.SMEM)] + [VMEM] * (pieces + 2) + [HBM],
+        functools.partial(late_kernel, slots[2:]),
+        out_shape=jax.ShapeDtypeStruct((local_res, columns, features), jnp.bfloat16),
+        in_specs=[smem] + [VMEM] * 5,
         out_specs=VMEM,
-        scratch_shapes=[
-            pltpu.VMEM((local_res * pieces * pitch, lanes), jnp.float32),
-            pltpu.VMEM((local_res * pieces * local_res, features), jnp.float32),
-            pltpu.VMEM((1, features), jnp.float32),
-            pltpu.SemaphoreType.DMA(()),
-        ],
-    )(place, *(near(v) for v in (left, *rights, out_weight)), out_bias.reshape(1, features))
+        scratch_shapes=[pltpu.VMEM((local_res * columns, features), jnp.float32)] + scratch,
+        name="late",
+    )(place, near(left_t), near(early), near(late), weight, near(bias))
 
 
 def swaps_fit(mesh):
-    res_shards, seq_shards = mesh.shape["res"], mesh.shape["seq"]
-    return seq_shards == 2 and res_shards in (2, 4, 8)
+    return mesh.shape["seq"] == 2 and mesh.shape["res"] == 8
 
 
 def solution(mesh):

time: 15.9 us -> 14.4 us (0.906)
  waiting for transfers between devices: 5.24 us -> 3.95 us
  starting transfers between devices: 7.45 us -> 7.21 us
    ppermute x4 -> x3, waiting for transfers between devices: 4.4 us -> 3.11 us  [send(): return lax.ppermute(value, ('res', 'seq'), pairs)]
    ppermute x4 -> x3, starting transfers between devices: 6.89 us -> 6.65 us  [send(): return lax.ppermute(value, ('res', 'seq'), pairs)]
    pallas_call x1 -> x2, Pallas kernels: 1.63 us -> 1.7 us  [the longest x1 1.04 us: on_device(): pl.pallas_call(functools.partial(late_kernel, slots[2:]), out_shape=jax.S...]
  transfers between devices with their start and end apart: 5 -> 4, of which waited for: 5 -> 4; matrix products, arithmetic and copies ran while one was open for 0% -> 0% of each run, Pallas kernels for 0% -> 5%
where the time goes in v3:
time: 14.4 us; the launch traced here: 14.2 us
  starting transfers between devices  7.21 us (50%)
  waiting for transfers between devices  3.95 us (27%)
  Pallas kernels  3.04 us (21%)
    ppermute x3, starting transfers between devices, send(): return lax.ppermute(value, ('res', 'seq'), pairs)  6.65 us
    ppermute x3, waiting for transfers between devices, send(): return lax.ppermute(value, ('res', 'seq'), pairs)  3.11 us
    pallas_call x1, Pallas kernels, on_device(): pl.pallas_call(project_kernel, out_shape=pltpu.VMEM((2, local_seqs, lanes...  1.34 us
    pallas_call x1, Pallas kernels, on_device(): pl.pallas_call(functools.partial(late_kernel, slots[2:]), out_shape=jax.S...  1.04 us
    ppermute x1, waiting for transfers between devices, on_device(): other = lax.ppermute(both, 'seq', [(0, 1), (1, 0)])  0.84 us
    pallas_call x1, Pallas kernels, on_device(): pl.pallas_call(functools.partial(early_kernel, local_res, slots[:2]), out...  0.66 us
    ppermute x1, starting transfers between devices, on_device(): other = lax.ppermute(both, 'seq', [(0, 1), (1, 0)])  0.56 us
  transfers between devices with their start and end apart: 4, of which 4 were waited for; matrix products, arithmetic and copies ran while one was open for 0% of the time, Pallas kernels for 5%

profile of v3, /device:TPU:0, one launch (start us, length us, event | category | flops | bytes accessed | tf_op | source)
XLA Modules:
  0.0 14.2 jit_solution(13264227537102657234)
XLA Ops:
  0.0 0.0 copy-start
  0.0 1.3 %shard_map.64 = bf16[2,32,128]{2,1,0:T(8,128)(2,1)S(1)} custom-call(bf16[32,4,256]{2,1,0:T(4,128)(2,1)} %x_hbm.1, f32[1,256]{1,0:T(1,128)} %bitcast.11, bf16[32,256]{1,0:T(8,128)(2,1)} %bitcast.9, bf16[32,256]{1,0:T(8,128)(2,1)} %bitcast.10), custom_call_target="tpu_custom_call" | custom-call | tf_op jit(solution)/shard_map/pallas_call | solution.py:178
  1.3 0.6 %collective-permute-start = (bf16[2,32,128]{2,1,0:T(8,128)(2,1)S(1)}, bf16[2,32,128]{2,1,0:T(8,128)(2,1)S(1)}, u32[]{:S(2)}, u32[]{:S(2)}) collective-permute-start(bf16[2,32,128]{2,1,0:T(8,128)(2,1)S(1)} %shard_map.64), channel_id=1, source_target_pairs={{0,1},{1,0},{2,3},{3,2},{4,5},{5,4},{6,7},{7,6},{8,9},{9,8},{10,11... | collective-permute-start | bytes 49160 | tf_op jit(solution)/shard_map/ppermute | solution.py:214
  1.9 0.8 %collective-permute-done = bf16[2,32,128]{2,1,0:T(8,128)(2,1)S(1)} collective-permute-done((bf16[2,32,128]{2,1,0:T(8,128)(2,1)S(1)}, bf16[2,32,128]{2,1,0:T(8,128)(2,1)S(1)}, u32[]{:S(2)}, u32[]{:S(2)}) %collective-permute-start) | collective-permute-done | bytes 16416 | tf_op jit(solution)/shard_map/ppermute | solution.py:214
  2.8 4.0 %collective-permute-start.1 = (bf16[64,128]{1,0:T(8,128)(2,1)S(1)}, bf16[64,128]{1,0:T(8,128)(2,1)S(1)}, u32[]{:S(2)}, u32[]{:S(2)}) collective-permute-start(bf16[64,128]{1,0:T(8,128)(2,1)S(1)} %get-tuple-element.11), channel_id=1, source_target_pairs={{0,8},{1,2},{2,10},{3,0},{4,12},{5,6},{6,14},{7,4},{8,1},{9,11},{1... | collective-permute-start | bytes 49160 | tf_op jit(solution)/shard_map/ppermute | solution.py:204
  6.7 1.0 %collective-permute-start.2 = (bf16[64,128]{1,0:T(8,128)(2,1)S(1)}, bf16[64,128]{1,0:T(8,128)(2,1)S(1)}, u32[]{:S(2)}, u32[]{:S(2)}) collective-permute-start(bf16[64,128]{1,0:T(8,128)(2,1)S(1)} %get-tuple-element.11), channel_id=1, source_target_pairs={{0,10},{1,0},{2,8},{3,2},{4,14},{5,4},{6,12},{7,6},{8,3},{9,11},{1... | collective-permute-start | bytes 49160 | tf_op jit(solution)/shard_map/ppermute | solution.py:204
  7.8 0.4 %collective-permute-done.1 = bf16[64,128]{1,0:T(8,128)(2,1)S(1)} collective-permute-done((bf16[64,128]{1,0:T(8,128)(2,1)S(1)}, bf16[64,128]{1,0:T(8,128)(2,1)S(1)}, u32[]{:S(2)}, u32[]{:S(2)}) %collective-permute-start.1) | collective-permute-done | bytes 16416 | tf_op jit(solution)/shard_map/ppermute | solution.py:204
  8.2 1.0 %collective-permute-done.2 = bf16[64,128]{1,0:T(8,128)(2,1)S(1)} collective-permute-done((bf16[64,128]{1,0:T(8,128)(2,1)S(1)}, bf16[64,128]{1,0:T(8,128)(2,1)S(1)}, u32[]{:S(2)}, u32[]{:S(2)}) %collective-permute-start.2) | collective-permute-done | bytes 16416 | tf_op jit(solution)/shard_map/ppermute | solution.py:204
  9.2 1.6 %collective-permute-start.3 = (bf16[128,128]{1,0:T(8,128)(2,1)S(1)}, bf16[128,128]{1,0:T(8,128)(2,1)S(1)}, u32[]{:S(2)}, u32[]{:S(2)}) collective-permute-start(bf16[128,128]{1,0:T(8,128)(2,1)S(1)} %pad_maximum_fusion.right_ref), channel_id=1, source_target_pairs={{0,4},{1,5},{2,6},{3,7},{4,0},{5,1},{6,2},{7,3},{8,12},{9,13},{10,... | collective-permute-start | bytes 98312 | tf_op jit(solution)/shard_map/ppermute | solution.py:204
  10.9 0.0 copy-done
  10.9 0.7 %early.1 = (bf16[128,64]{1,0:T(8,128)(2,1)S(1)}, f32[64,128]{1,0:T(8,128)S(1)}, f32[1,128]{1,0:T(1,128)S(1)}) custom-call(s32[1]{0:T(128)} %bitcast.place_ref, bf16[64,128]{1,0:T(8,128)(2,1)S(1)} %get-tuple-element.12.left_ref, bf16[128,128]{1,0:T(8,128)(2,1)S(1)} %pad_maximum_fusion.right_ref, bf16[1024,128]{1,0:T(8,128)(2,1)S(1)} %copy-done, f32[1,128]{1,0:T(1,128)} %bitcast.12), custom_call_target="tpu_custom_call" | custom-call | flops 1000000000 | tf_op jit(solution)/shard_map/early/pallas_call | solution.py:235
  11.5 1.7 %collective-permute-done.3.right_ref = bf16[128,128]{1,0:T(8,128)(2,1)S(1)} collective-permute-done((bf16[128,128]{1,0:T(8,128)(2,1)S(1)}, bf16[128,128]{1,0:T(8,128)(2,1)S(1)}, u32[]{:S(2)}, u32[]{:S(2)}) %collective-permute-start.3) | collective-permute-done | bytes 32800 | tf_op jit(solution)/shard_map/ppermute | solution.py:204
  13.2 1.0 %late.1 = bf16[4,16,128]{2,1,0:T(8,128)(2,1)} custom-call(s32[1]{0:T(128)} %bitcast.place_ref, bf16[128,64]{1,0:T(8,128)(2,1)S(1)} %get-tuple-element.8.left_t_ref, f32[64,128]{1,0:T(8,128)S(1)} %get-tuple-element.9.early_ref, bf16[128,128]{1,0:T(8,128)(2,1)S(1)} %collective-permute-done.3.right_ref, bf16[1024,128]{1,0:T(8,128)(2,1)S(1)} %copy-done, ...), custom_call_target="tpu_custom_call" | custom-call | tf_op jit(solution)/shard_map/late/pallas_call | solution.py:248
  (4 shorter events, 0.0 us)
Async XLA Ops:
  0.0 10.9 %copy-start = (bf16[1024,128]{1,0:T(8,128)(2,1)S(1)}, bf16[1024,128]{1,0:T(8,128)(2,1)}, u32[]{:S(2)}) copy-start(bf16[1024,128]{1,0:T(8,128)(2,1)} %weight_ref.3) | copy-start | bytes 786436
  1.3 1.4 %collective-permute-start = (bf16[2,32,128]{2,1,0:T(8,128)(2,1)S(1)}, bf16[2,32,128]{2,1,0:T(8,128)(2,1)S(1)}, u32[]{:S(2)}, u32[]{:S(2)}) collective-permute-start(bf16[2,32,128]{2,1,0:T(8,128)(2,1)S(1)} %shard_map.64), channel_id=1, source_target_pairs={{0,1},{1,0},{2,3},{3,2},{4,5},{5,4},{6,7},{7,6},{8,9},{9,8},{10,11... | collective-permute-start | bytes 49160 | tf_op jit(solution)/shard_map/ppermute | solution.py:214
  2.8 5.4 %collective-permute-start.1 = (bf16[64,128]{1,0:T(8,128)(2,1)S(1)}, bf16[64,128]{1,0:T(8,128)(2,1)S(1)}, u32[]{:S(2)}, u32[]{:S(2)}) collective-permute-start(bf16[64,128]{1,0:T(8,128)(2,1)S(1)} %get-tuple-element.11), channel_id=1, source_target_pairs={{0,8},{1,2},{2,10},{3,0},{4,12},{5,6},{6,14},{7,4},{8,1},{9,11},{1... | collective-permute-start | bytes 49160 | tf_op jit(solution)/shard_map/ppermute | solution.py:204
  6.7 2.5 %collective-permute-start.2 = (bf16[64,128]{1,0:T(8,128)(2,1)S(1)}, bf16[64,128]{1,0:T(8,128)(2,1)S(1)}, u32[]{:S(2)}, u32[]{:S(2)}) collective-permute-start(bf16[64,128]{1,0:T(8,128)(2,1)S(1)} %get-tuple-element.11), channel_id=1, source_target_pairs={{0,10},{1,0},{2,8},{3,2},{4,14},{5,4},{6,12},{7,6},{8,3},{9,11},{1... | collective-permute-start | bytes 49160 | tf_op jit(solution)/shard_map/ppermute | solution.py:204
  9.2 4.0 %collective-permute-start.3 = (bf16[128,128]{1,0:T(8,128)(2,1)S(1)}, bf16[128,128]{1,0:T(8,128)(2,1)S(1)}, u32[]{:S(2)}, u32[]{:S(2)}) collective-permute-start(bf16[128,128]{1,0:T(8,128)(2,1)S(1)} %pad_maximum_fusion.right_ref), channel_id=1, source_target_pairs={{0,4},{1,5},{2,6},{3,7},{4,0},{5,1},{6,2},{7,3},{8,12},{9,13},{10,... | collective-permute-start | bytes 98312 | tf_op jit(solution)/shard_map/ppermute | solution.py:204

commit v4 on v3

--- a/solution.py
+++ b/solution.py
@@ -114,12 +114,14 @@
         both_ref[n] = jnp.concatenate(side, axis=1).astype(jnp.bfloat16)
 
 
-def pair_rows(left_t, pieces, places, local_res, weight_ref, terms, totals, rows):
-    count = local_res * len(pieces)
-    channels = left_t.shape[0] // local_res
-    lanes = pieces[0].shape[1]
+def pair_rows(left_t_ref, pairs, places, local_res, weight_ref, terms, totals, rows):
+    left_t = left_t_ref[...]
+    lanes, seqs = left_t.shape
+    count = local_res * len(places)
+    channels = lanes // local_res
     per_piece = lanes // channels
-    pitch = terms.shape[0] // count
+    pitch = channels + 8
+    pieces = [ref[first : first + seqs] for ref in pairs for first in range(0, ref.shape[0], seqs)]
     for n, piece in enumerate(pieces):
         product = jnp.dot(left_t, piece, preferred_element_type=jnp.float32)
         for i in range(local_res):
@@ -134,7 +136,9 @@
     weight = jnp.concatenate(
         [weight_ref[c * channels : (c + 1) * channels] for c in range(channels) for _ in range(per_piece)], axis=0
     )
-    totals[...] = jnp.dot(jnp.concatenate(spread, axis=1), weight, preferred_element_type=jnp.float32)
+    totals[: count * per_piece, :] = jnp.dot(
+        jnp.concatenate(spread, axis=1), weight, preferred_element_type=jnp.float32
+    )
     columns = rows.shape[0] // local_res
     for n, at in enumerate(places):
         for j in range(per_piece):
@@ -143,28 +147,35 @@
 
 
 def early_kernel(
-    local_res, slots, place_ref, left_ref, right_ref, weight_ref, bias_hbm, left_t_ref, rows, bias_ref, terms, totals, sem
+    local_res, step, home_ref, low_ref, from_ref, left_ref, own_ref, one_ref, weight_ref, bias_hbm, left_t_ref, rows, bias_ref, terms, totals, sem
 ):
     bias_copy = pltpu.make_async_copy(bias_hbm, bias_ref, sem)
     bias_copy.start()
     left_t_ref[...] = left_ref[...].T
-    seqs = left_ref.shape[0]
-    pieces = [right_ref[n * seqs : (n + 1) * seqs] for n in range(len(slots))]
-    places = [place_ref[0] ^ slot for slot in slots]
     rows[...] = jnp.zeros_like(rows)
-    pair_rows(left_t_ref[...], pieces, places, local_res, weight_ref, terms, totals, rows)
+    home, low, arrived = home_ref[0], low_ref[0], from_ref[0]
+
+    @pl.when(home == 1)
+    def _():
+        places = [low, low ^ step, arrived, arrived ^ step]
+        pair_rows(left_t_ref, (own_ref, one_ref), places, local_res, weight_ref, terms, totals, rows)
+
+    @pl.when(home == 0)
+    def _():
+        pair_rows(left_t_ref, (one_ref,), [arrived, arrived ^ step], local_res, weight_ref, terms, totals, rows)
+
     bias_copy.wait()
 
 
-def late_kernel(
-    slots, place_ref, left_t_ref, early_ref, right_ref, weight_ref, bias_ref, out_ref, rows, terms, totals
-):
+def late_kernel(step, home_ref, from_ref, left_t_ref, early_ref, two_ref, weight_ref, bias_ref, out_ref, rows, terms, totals):
     rows[...] = early_ref[...]
-    seqs = left_t_ref.shape[1]
-    pieces = [right_ref[n * seqs : (n + 1) * seqs] for n in range(len(slots))]
-    places = [place_ref[0] ^ slot for slot in slots]
-    pair_rows(left_t_ref[...], pieces, places, out_ref.shape[0], weight_ref, terms, totals, rows)
-    total = rows[...] * (1.0 / seqs) + bias_ref[...]
+
+    @pl.when(home_ref[0] == 0)
+    def _():
+        arrived = from_ref[0]
+        pair_rows(left_t_ref, (two_ref,), [arrived, arrived ^ step], out_ref.shape[0], weight_ref, terms, totals, rows)
+
+    total = rows[...] * (1.0 / left_t_ref.shape[1]) + bias_ref[...]
     out_ref[...] = total.reshape(out_ref.shape).astype(out_ref.dtype)
 
 
@@ -203,56 +214,63 @@
                 pairs.append((r * seq_shards + q, to_res * seq_shards + to_seq))
         return lax.ppermute(value, ("res", "seq"), pairs)
 
-    def flow(far, near_by):
-        def target(r, q):
-            if q == 0:
-                return r ^ half ^ far, int(r >= half)
-            return (r ^ 1, 1) if r >= half else (r ^ near_by, 0)
-
-        return target
-
     other = lax.ppermute(both, "seq", [(0, 1), (1, 0)])
     first = seq == 0
     full = jnp.concatenate((jnp.where(first, both, other), jnp.where(first, other, both)), axis=1)
     left, right = full[0], full[1]
     home = res // half == seq
-    one = send(right, flow(0, 1))
-    two = send(right, flow(1, 0))
-    mine = jnp.concatenate((jnp.where(home, right, one), jnp.where(home, one, two)), 0)
-    late = send(mine, lambda r, q: (r ^ 2, q))
-    slots = (0, 1, 2, 3)
+
+    def flow(served, offsets):
+        def target(r, q):
+            k = r // half * 2 + q
+            return served[k] // 2 * half + (r % half ^ offsets[k]), served[k] % 2
+
+        return target
+
+    cross = flow((1, 0, 3, 2), (1, 1, 1, 1))
+    round_one = flow((2, 0, 3, 1), (0, 2, 2, 2))
+    round_two = flow((2, 0, 3, 1), (2, 0, 0, 0))
+    pair = jnp.concatenate((right, send(right, cross)), 0)
+    one = send(pair, round_one)
+    two = send(pair, round_two)
+    low = res % half
+    served_from_lower = jnp.logical_and(res >= half, seq == 0)
+    from_one_value = low ^ jnp.where(served_from_lower, 0, 2)
+    from_two_value = low ^ jnp.where(served_from_lower, 2, 0)
+    at_home = home.astype(jnp.int32).reshape(1)
+    from_one = from_one_value.reshape(1)
+    from_two = from_two_value.reshape(1)
     nseq = right.shape[0]
-    place = (res % half).reshape(1)
     weight = near(out_weight)
     columns = pieces * local_res
     pitch = channels + 8
-    count = local_res * 2
+    count = local_res * pieces
     smem = pl.BlockSpec(memory_space=pltpu.SMEM)
     scratch = [
         pltpu.VMEM((count * pitch, lanes), jnp.float32),
         pltpu.VMEM((count * local_res, features), jnp.float32),
     ]
     left_t, early, bias = pl.pallas_call(
-        functools.partial(early_kernel, local_res, slots[:2]),
+        functools.partial(early_kernel, local_res, 1),
         out_shape=[
             pltpu.VMEM((lanes, nseq), jnp.bfloat16),
             pltpu.VMEM((local_res * columns, features), jnp.float32),
             pltpu.VMEM((1, features), jnp.float32),
         ],
-        in_specs=[smem] + [VMEM] * 3 + [HBM],
+        in_specs=[smem] * 3 + [VMEM] * 4 + [HBM],
         out_specs=[VMEM] * 3,
         scratch_shapes=scratch + [pltpu.SemaphoreType.DMA(())],
         cost_estimate=pl.CostEstimate(flops=10**9, transcendentals=0, bytes_accessed=0),
         name="early",
-    )(place, near(left), near(mine), weight, out_bias.reshape(1, features))
+    )(at_home, low.reshape(1), from_one, near(left), near(pair), near(one), weight, out_bias.reshape(1, features))
     return pl.pallas_call(
-        functools.partial(late_kernel, slots[2:]),
+        functools.partial(late_kernel, 1),
         out_shape=jax.ShapeDtypeStruct((local_res, columns, features), jnp.bfloat16),
-        in_specs=[smem] + [VMEM] * 5,
+        in_specs=[smem] * 2 + [VMEM] * 5,
         out_specs=VMEM,
         scratch_shapes=[pltpu.VMEM((local_res * columns, features), jnp.float32)] + scratch,
         name="late",
-    )(place, near(left_t), near(early), near(late), weight, near(bias))
+    )(at_home, from_two, near(left_t), near(early), near(two), weight, near(bias))
 
 
 def swaps_fit(mesh):

time: 14.4 us -> 13.6 us (0.944)
  waiting for transfers between devices: 3.95 us -> 3.21 us
  Pallas kernels: 3.04 us -> 2.62 us
  starting transfers between devices: 7.21 us -> 7.49 us
    ppermute x3, waiting for transfers between devices: 3.11 us -> 2.37 us  [send(): return lax.ppermute(value, ('res', 'seq'), pairs)]
    pallas_call x2, Pallas kernels: 1.7 us -> 1.28 us  [the longest x1 0.66 us: on_device(): pl.pallas_call(functools.partial(early_kernel, local_res, 1), out_shape=[...]
    ppermute x3, starting transfers between devices: 6.65 us -> 6.93 us  [send(): return lax.ppermute(value, ('res', 'seq'), pairs)]
where the time goes in v4:
time: 13.6 us; the launch traced here: 13.4 us
  starting transfers between devices  7.49 us (55%)
  waiting for transfers between devices  3.21 us (24%)
  Pallas kernels  2.62 us (19%)
    ppermute x3, starting transfers between devices, send(): return lax.ppermute(value, ('res', 'seq'), pairs)  6.93 us
    ppermute x3, waiting for transfers between devices, send(): return lax.ppermute(value, ('res', 'seq'), pairs)  2.37 us
    pallas_call x1, Pallas kernels, on_device(): pl.pallas_call(project_kernel, out_shape=pltpu.VMEM((2, local_seqs, lanes...  1.34 us
    ppermute x1, waiting for transfers between devices, on_device(): other = lax.ppermute(both, 'seq', [(0, 1), (1, 0)])  0.84 us
    pallas_call x1, Pallas kernels, on_device(): pl.pallas_call(functools.partial(early_kernel, local_res, 1), out_shape=[...  0.66 us
    pallas_call x1, Pallas kernels, on_device(): pl.pallas_call(functools.partial(late_kernel, 1), out_shape=jax.ShapeDtyp...  0.62 us
    ppermute x1, starting transfers between devices, on_device(): other = lax.ppermute(both, 'seq', [(0, 1), (1, 0)])  0.56 us
  transfers between devices with their start and end apart: 4, of which 4 were waited for; matrix products, arithmetic and copies ran while one was open for 0% of the time, Pallas kernels for 5%

profile of v4, /device:TPU:0, one launch (start us, length us, event | category | flops | bytes accessed | tf_op | source)
XLA Modules:
  0.0 13.4 jit_solution(6143154922691298623)
XLA Ops:
  0.0 0.0 copy-start
  0.0 1.3 %shard_map.64 = bf16[2,32,128]{2,1,0:T(8,128)(2,1)S(1)} custom-call(bf16[32,4,256]{2,1,0:T(4,128)(2,1)} %x_hbm.1, f32[1,256]{1,0:T(1,128)} %bitcast.14, bf16[32,256]{1,0:T(8,128)(2,1)} %bitcast.12, bf16[32,256]{1,0:T(8,128)(2,1)} %bitcast.13), custom_call_target="tpu_custom_call" | custom-call | tf_op jit(solution)/shard_map/pallas_call | solution.py:189
  1.3 0.6 %collective-permute-start = (bf16[2,32,128]{2,1,0:T(8,128)(2,1)S(1)}, bf16[2,32,128]{2,1,0:T(8,128)(2,1)S(1)}, u32[]{:S(2)}, u32[]{:S(2)}) collective-permute-start(bf16[2,32,128]{2,1,0:T(8,128)(2,1)S(1)} %shard_map.64), channel_id=1, source_target_pairs={{0,1},{1,0},{2,3},{3,2},{4,5},{5,4},{6,7},{7,6},{8,9},{9,8},{10,11... | collective-permute-start | bytes 49160 | tf_op jit(solution)/shard_map/ppermute | solution.py:217
  1.9 0.8 %collective-permute-done = bf16[2,32,128]{2,1,0:T(8,128)(2,1)S(1)} collective-permute-done((bf16[2,32,128]{2,1,0:T(8,128)(2,1)S(1)}, bf16[2,32,128]{2,1,0:T(8,128)(2,1)S(1)}, u32[]{:S(2)}, u32[]{:S(2)}) %collective-permute-start) | collective-permute-done | bytes 16416 | tf_op jit(solution)/shard_map/ppermute | solution.py:217
  2.8 2.7 %collective-permute-start.1 = (bf16[64,128]{1,0:T(8,128)(2,1)S(1)}, bf16[64,128]{1,0:T(8,128)(2,1)S(1)}, u32[]{:S(2)}, u32[]{:S(2)}) collective-permute-start(bf16[64,128]{1,0:T(8,128)(2,1)S(1)} %get-tuple-element.11), channel_id=1, source_target_pairs={{0,3},{1,2},{2,1},{3,0},{4,7},{5,6},{6,5},{7,4},{8,11},{9,10},{10,... | collective-permute-start | bytes 49160 | tf_op jit(solution)/shard_map/ppermute | solution.py:215
  5.4 1.4 %collective-permute-done.1 = bf16[64,128]{1,0:T(8,128)(2,1)S(1)} collective-permute-done((bf16[64,128]{1,0:T(8,128)(2,1)S(1)}, bf16[64,128]{1,0:T(8,128)(2,1)S(1)}, u32[]{:S(2)}, u32[]{:S(2)}) %collective-permute-start.1) | collective-permute-done | bytes 16416 | tf_op jit(solution)/shard_map/ppermute | solution.py:215
  6.9 3.0 %collective-permute-start.2 = (bf16[128,128]{1,0:T(8,128)(2,1)S(1)}, bf16[128,128]{1,0:T(8,128)(2,1)S(1)}, u32[]{:S(2)}, u32[]{:S(2)}) collective-permute-start(bf16[128,128]{1,0:T(8,128)(2,1)S(1)} %pad_maximum_fusion.own_ref), channel_id=1, source_target_pairs={{0,8},{1,4},{2,10},{3,6},{4,12},{5,0},{6,14},{7,2},{8,13},{9,5},{1... | collective-permute-start | bytes 98312 | tf_op jit(solution)/shard_map/ppermute | solution.py:215
  9.9 1.2 %collective-permute-start.3 = (bf16[128,128]{1,0:T(8,128)(2,1)S(1)}, bf16[128,128]{1,0:T(8,128)(2,1)S(1)}, u32[]{:S(2)}, u32[]{:S(2)}) collective-permute-start(bf16[128,128]{1,0:T(8,128)(2,1)S(1)} %pad_maximum_fusion.own_ref), channel_id=1, source_target_pairs={{0,12},{1,0},{2,14},{3,2},{4,8},{5,4},{6,10},{7,6},{8,9},{9,1},{10... | collective-permute-start | bytes 98312 | tf_op jit(solution)/shard_map/ppermute | solution.py:215
  11.1 0.4 %collective-permute-done.2.one_ref = bf16[128,128]{1,0:T(8,128)(2,1)S(1)} collective-permute-done((bf16[128,128]{1,0:T(8,128)(2,1)S(1)}, bf16[128,128]{1,0:T(8,128)(2,1)S(1)}, u32[]{:S(2)}, u32[]{:S(2)}) %collective-permute-start.2) | collective-permute-done | bytes 32800 | tf_op jit(solution)/shard_map/ppermute | solution.py:215
  11.5 0.0 copy-done
  11.5 0.7 %early.1 = (bf16[128,64]{1,0:T(8,128)(2,1)S(1)}, f32[64,128]{1,0:T(8,128)S(1)}, f32[1,128]{1,0:T(1,128)S(1)}) custom-call(s32[1]{0:T(128)} %bitcast.home_ref, s32[1]{0:T(128)} %bitcast.2.low_ref, s32[1]{0:T(128)} %bitcast.3.from_ref, bf16[64,128]{1,0:T(8,128)(2,1)S(1)} %get-tuple-element.12.left_ref, bf16[128,128]{1,0:T(8,128)(2,1)S(1)} %pad_maximum_fusion.own_ref, ...), custom_call_target="tpu_custom_call" | custom-call | flops 1000000000 | tf_op jit(solution)/shard_map/early/pallas_call | solution.py:253
  12.2 0.6 %collective-permute-done.3.two_ref = bf16[128,128]{1,0:T(8,128)(2,1)S(1)} collective-permute-done((bf16[128,128]{1,0:T(8,128)(2,1)S(1)}, bf16[128,128]{1,0:T(8,128)(2,1)S(1)}, u32[]{:S(2)}, u32[]{:S(2)}) %collective-permute-start.3) | collective-permute-done | bytes 32800 | tf_op jit(solution)/shard_map/ppermute | solution.py:215
  12.7 0.6 %late.1 = bf16[4,16,128]{2,1,0:T(8,128)(2,1)} custom-call(s32[1]{0:T(128)} %bitcast.home_ref, s32[1]{0:T(128)} %bitcast.1.from_ref, bf16[128,64]{1,0:T(8,128)(2,1)S(1)} %get-tuple-element.8.left_t_ref, f32[64,128]{1,0:T(8,128)S(1)} %get-tuple-element.9.early_ref, bf16[128,128]{1,0:T(8,128)(2,1)S(1)} %collective-permute-done.3.two_ref, ...), custom_call_target="tpu_custom_call" | custom-call | tf_op jit(solution)/shard_map/late/pallas_call | solution.py:266
  (3 shorter events, 0.0 us)
Async XLA Ops:
  0.0 11.5 %copy-start = (bf16[1024,128]{1,0:T(8,128)(2,1)S(1)}, bf16[1024,128]{1,0:T(8,128)(2,1)}, u32[]{:S(2)}) copy-start(bf16[1024,128]{1,0:T(8,128)(2,1)} %weight_ref.3) | copy-start | bytes 786436
  1.3 1.4 %collective-permute-start = (bf16[2,32,128]{2,1,0:T(8,128)(2,1)S(1)}, bf16[2,32,128]{2,1,0:T(8,128)(2,1)S(1)}, u32[]{:S(2)}, u32[]{:S(2)}) collective-permute-start(bf16[2,32,128]{2,1,0:T(8,128)(2,1)S(1)} %shard_map.64), channel_id=1, source_target_pairs={{0,1},{1,0},{2,3},{3,2},{4,5},{5,4},{6,7},{7,6},{8,9},{9,8},{10,11... | collective-permute-start | bytes 49160 | tf_op jit(solution)/shard_map/ppermute | solution.py:217
  2.8 4.1 %collective-permute-start.1 = (bf16[64,128]{1,0:T(8,128)(2,1)S(1)}, bf16[64,128]{1,0:T(8,128)(2,1)S(1)}, u32[]{:S(2)}, u32[]{:S(2)}) collective-permute-start(bf16[64,128]{1,0:T(8,128)(2,1)S(1)} %get-tuple-element.11), channel_id=1, source_target_pairs={{0,3},{1,2},{2,1},{3,0},{4,7},{5,6},{6,5},{7,4},{8,11},{9,10},{10,... | collective-permute-start | bytes 49160 | tf_op jit(solution)/shard_map/ppermute | solution.py:215
  6.9 4.6 %collective-permute-start.2 = (bf16[128,128]{1,0:T(8,128)(2,1)S(1)}, bf16[128,128]{1,0:T(8,128)(2,1)S(1)}, u32[]{:S(2)}, u32[]{:S(2)}) collective-permute-start(bf16[128,128]{1,0:T(8,128)(2,1)S(1)} %pad_maximum_fusion.own_ref), channel_id=1, source_target_pairs={{0,8},{1,4},{2,10},{3,6},{4,12},{5,0},{6,14},{7,2},{8,13},{9,5},{1... | collective-permute-start | bytes 98312 | tf_op jit(solution)/shard_map/ppermute | solution.py:215
  9.9 2.8 %collective-permute-start.3 = (bf16[128,128]{1,0:T(8,128)(2,1)S(1)}, bf16[128,128]{1,0:T(8,128)(2,1)S(1)}, u32[]{:S(2)}, u32[]{:S(2)}) collective-permute-start(bf16[128,128]{1,0:T(8,128)(2,1)S(1)} %pad_maximum_fusion.own_ref), channel_id=1, source_target_pairs={{0,12},{1,0},{2,14},{3,2},{4,8},{5,4},{6,10},{7,6},{8,9},{9,1},{10... | collective-permute-start | bytes 98312 | tf_op jit(solution)/shard_map/ppermute | solution.py:215

commit v5 on v4

--- a/solution.py
+++ b/solution.py
@@ -78,11 +78,15 @@
     return pltpu.with_memory_space_constraint(value, pltpu.VMEM)
 
 
-def project_kernel(x_hbm, gain_hbm, left_hbm, right_hbm, both_ref, x_ref, gain_ref, left_ref, right_ref, rows, sems):
+def project_kernel(
+    x_hbm, gain_hbm, left_hbm, right_hbm, bias_hbm, both_ref, bias_ref, x_ref, gain_ref, left_ref, right_ref, rows, sems
+):
     copies = [
         pltpu.make_async_copy(source, target, sems.at[n])
         for n, (source, target) in enumerate(
-            ((x_hbm, x_ref), (gain_hbm, gain_ref), (left_hbm, left_ref), (right_hbm, right_ref))
+            (
+                (x_hbm, x_ref), (gain_hbm, gain_ref), (left_hbm, left_ref), (right_hbm, right_ref), (bias_hbm, bias_ref)
+            )
         )
     ]
     for copy in copies:
@@ -93,7 +97,7 @@
     for n in range(tiles):
         part = x_ref[:, :, n * lanes : (n + 1) * lanes].astype(jnp.float32)
         rows[n] = part.reshape(seqs * local_res, lanes)
-    for copy in copies[1:]:
+    for copy in copies[1:-1]:
         copy.wait()
     sides = ([], [])
     for r in range(local_res):
@@ -112,6 +116,7 @@
             )
     for n, side in enumerate(sides):
         both_ref[n] = jnp.concatenate(side, axis=1).astype(jnp.bfloat16)
+    copies[-1].wait()
 
 
 def pair_rows(left_t_ref, pairs, places, local_res, weight_ref, terms, totals, rows):
@@ -146,37 +151,48 @@
             rows[pl.ds(at * per_piece + j, local_res, stride=columns), :] = row
 
 
+def turn_kernel(left_ref, left_t_ref):
+    left_t_ref[...] = left_ref[...].T
+
+
+def write_out(rows, inv_count, bias_ref, out_hbm, packed, sem):
+    total = rows[...] * inv_count + bias_ref[...]
+    packed[...] = total.reshape(packed.shape).astype(packed.dtype)
+    copy = pltpu.make_async_copy(packed, out_hbm, sem)
+    copy.start()
+    copy.wait()
+
+
 def early_kernel(
-    local_res, step, home_ref, low_ref, from_ref, left_ref, own_ref, one_ref, weight_ref, bias_hbm, left_t_ref, rows, bias_ref, terms, totals, sem
+    step, home_ref, low_ref, one_at_ref, left_t_ref, own_ref, one_ref, weight_ref, bias_ref,
+    out_hbm, rows, terms, totals, packed, sem
 ):
-    bias_copy = pltpu.make_async_copy(bias_hbm, bias_ref, sem)
-    bias_copy.start()
-    left_t_ref[...] = left_ref[...].T
-    rows[...] = jnp.zeros_like(rows)
-    home, low, arrived = home_ref[0], low_ref[0], from_ref[0]
-
-    @pl.when(home == 1)
+    low, one_at = low_ref[0], one_at_ref[0]
+    local_res = packed.shape[0]
+
+    @pl.when(home_ref[0] == 1)
     def _():
-        places = [low, low ^ step, arrived, arrived ^ step]
+        places = [low, low ^ step, one_at, one_at ^ step]
         pair_rows(left_t_ref, (own_ref, one_ref), places, local_res, weight_ref, terms, totals, rows)
-
-    @pl.when(home == 0)
-    def _():
-        pair_rows(left_t_ref, (one_ref,), [arrived, arrived ^ step], local_res, weight_ref, terms, totals, rows)
-
-    bias_copy.wait()
-
-
-def late_kernel(step, home_ref, from_ref, left_t_ref, early_ref, two_ref, weight_ref, bias_ref, out_ref, rows, terms, totals):
-    rows[...] = early_ref[...]
+        write_out(rows, 1.0 / left_t_ref.shape[1], bias_ref, out_hbm, packed, sem)
 
     @pl.when(home_ref[0] == 0)
     def _():
-        arrived = from_ref[0]
-        pair_rows(left_t_ref, (two_ref,), [arrived, arrived ^ step], out_ref.shape[0], weight_ref, terms, totals, rows)
-
-    total = rows[...] * (1.0 / left_t_ref.shape[1]) + bias_ref[...]
-    out_ref[...] = total.reshape(out_ref.shape).astype(out_ref.dtype)
+        rows[...] = jnp.zeros_like(rows)
+        pair_rows(left_t_ref, (one_ref,), [one_at, one_at ^ step], local_res, weight_ref, terms, totals, rows)
+
+
+def late_kernel(
+    step, home_ref, two_at_ref, left_t_ref, two_ref, weight_ref, bias_ref, early_rows, early_hbm,
+    out_hbm, rows, terms, totals, packed, sem
+):
+    two_at = two_at_ref[0]
+
+    @pl.when(home_ref[0] == 0)
+    def _():
+        rows[...] = early_rows[...]
+        pair_rows(left_t_ref, (two_ref,), [two_at, two_at ^ step], packed.shape[0], weight_ref, terms, totals, rows)
+        write_out(rows, 1.0 / left_t_ref.shape[1], bias_ref, out_hbm, packed, sem)
 
 
 def on_device(alignment, ln_gain, proj_left, proj_right, out_weight, out_bias):
@@ -186,20 +202,24 @@
     channels = proj_left.shape[1]
     lanes = local_res * channels
     features = out_weight.shape[1]
-    both = pl.pallas_call(
+    both, bias = pl.pallas_call(
         project_kernel,
-        out_shape=pltpu.VMEM((2, local_seqs, lanes), jnp.bfloat16),
-        in_specs=[HBM] * 4,
-        out_specs=VMEM,
+        out_shape=[
+            pltpu.VMEM((2, local_seqs, lanes), jnp.bfloat16),
+            pltpu.VMEM((1, features), jnp.float32),
+        ],
+        in_specs=[HBM] * 5,
+        out_specs=[VMEM] * 2,
         scratch_shapes=[
             pltpu.VMEM(alignment.shape, alignment.dtype),
             pltpu.VMEM((1, width), jnp.float32),
             pltpu.VMEM((channels, width), proj_left.dtype),
             pltpu.VMEM((channels, width), proj_right.dtype),
             pltpu.VMEM((width // 128, local_seqs * local_res, 128), jnp.float32),
-            pltpu.SemaphoreType.DMA((4,)),
+            pltpu.SemaphoreType.DMA((5,)),
         ],
-    )(alignment, ln_gain.reshape(1, width), proj_left.T, proj_right.T)
+        name="project",
+    )(alignment, ln_gain.reshape(1, width), proj_left.T, proj_right.T, out_bias.reshape(1, features))
 
     pieces = res_shards // seq_shards
     res = lax.axis_index("res")
@@ -238,39 +258,48 @@
     from_one_value = low ^ jnp.where(served_from_lower, 0, 2)
     from_two_value = low ^ jnp.where(served_from_lower, 2, 0)
     at_home = home.astype(jnp.int32).reshape(1)
-    from_one = from_one_value.reshape(1)
-    from_two = from_two_value.reshape(1)
-    nseq = right.shape[0]
+    one_at = from_one_value.reshape(1)
+    two_at = from_two_value.reshape(1)
     weight = near(out_weight)
+    bias = near(bias)
     columns = pieces * local_res
-    pitch = channels + 8
     count = local_res * pieces
     smem = pl.BlockSpec(memory_space=pltpu.SMEM)
+    out = jax.ShapeDtypeStruct((local_res, columns, features), jnp.bfloat16)
+    rows = pltpu.VMEM((local_res * columns, features), jnp.float32)
     scratch = [
-        pltpu.VMEM((count * pitch, lanes), jnp.float32),
+        pltpu.VMEM((count * (channels + 8), lanes), jnp.float32),
         pltpu.VMEM((count * local_res, features), jnp.float32),
+        pltpu.VMEM(out.shape, out.dtype),
+        pltpu.SemaphoreType.DMA(()),
     ]
-    left_t, early, bias = pl.pallas_call(
-        functools.partial(early_kernel, local_res, 1),
-        out_shape=[
-            pltpu.VMEM((lanes, nseq), jnp.bfloat16),
-            pltpu.VMEM((local_res * columns, features), jnp.float32),
-            pltpu.VMEM((1, features), jnp.float32),
-        ],
-        in_specs=[smem] * 3 + [VMEM] * 4 + [HBM],
-        out_specs=[VMEM] * 3,
-        scratch_shapes=scratch + [pltpu.SemaphoreType.DMA(())],
+    left_t = near(
+        pl.pallas_call(
+            turn_kernel,
+            out_shape=pltpu.VMEM((lanes, left.shape[0]), jnp.bfloat16),
+            in_specs=[VMEM],
+            out_specs=VMEM,
+            name="turn",
+        )(near(left))
+    )
+    early, early_rows = pl.pallas_call(
+        functools.partial(early_kernel, 1),
+        out_shape=[out, rows],
+        in_specs=[smem] * 3 + [VMEM] * 5,
+        out_specs=[HBM, VMEM],
+        scratch_shapes=scratch,
         cost_estimate=pl.CostEstimate(flops=10**9, transcendentals=0, bytes_accessed=0),
         name="early",
-    )(at_home, low.reshape(1), from_one, near(left), near(pair), near(one), weight, out_bias.reshape(1, features))
+    )(at_home, low.reshape(1), one_at, left_t, near(pair), near(one), weight, bias)
     return pl.pallas_call(
         functools.partial(late_kernel, 1),
-        out_shape=jax.ShapeDtypeStruct((local_res, columns, features), jnp.bfloat16),
-        in_specs=[smem] * 2 + [VMEM] * 5,
-        out_specs=VMEM,
-        scratch_shapes=[pltpu.VMEM((local_res * columns, features), jnp.float32)] + scratch,
+        out_shape=out,
+        in_specs=[smem] * 2 + [VMEM] * 5 + [HBM],
+        out_specs=HBM,
+        scratch_shapes=[rows] + scratch,
+        input_output_aliases={7: 0},
         name="late",
-    )(at_home, from_two, near(left_t), near(early), near(two), weight, near(bias))
+    )(at_home, two_at, left_t, near(two), weight, bias, near(early_rows), early)
 
 
 def swaps_fit(mesh):

time: 13.6 us -> 13.5 us (level)
  the two profiles are of different devices: /device:TPU:0 before, /device:TPU:1 now
where the time goes in v5:
time: 13.5 us; the launch traced here: 13.4 us
  starting transfers between devices  6.03 us (45%)
  waiting for transfers between devices  4.4 us (33%)
  Pallas kernels  2.9 us (21%)
    ppermute x3, starting transfers between devices, send(): return lax.ppermute(value, ('res', 'seq'), pairs)  5.95 us
    ppermute x3, waiting for transfers between devices, send(): return lax.ppermute(value, ('res', 'seq'), pairs)  3.23 us
    pallas_call x1, Pallas kernels, on_device(): pl.pallas_call(project_kernel, out_shape=[pltpu.VMEM((2, local_seqs, lane...  1.35 us
    ppermute x1, waiting for transfers between devices, on_device(): other = lax.ppermute(both, 'seq', [(0, 1), (1, 0)])  1.16 us
    pallas_call x1, Pallas kernels, on_device(): pl.pallas_call(functools.partial(late_kernel, 1), out_shape=out, in_specs...  1.05 us
    pallas_call x1, Pallas kernels, on_device(): pl.pallas_call(functools.partial(early_kernel, 1), out_shape=[out, rows],...  0.44 us
  transfers between devices with their start and end apart: 4, of which 4 were waited for; matrix products, arithmetic and copies ran while one was open for 0% of the time, Pallas kernels for 4%

profile of v5, /device:TPU:1, one launch (start us, length us, event | category | flops | bytes accessed | tf_op | source)
XLA Modules:
  0.0 13.4 jit_solution(14004421062266390386)
XLA Ops:
  0.0 0.0 copy-start
  0.0 1.3 %project.1 = (bf16[2,32,128]{2,1,0:T(8,128)(2,1)S(1)}, f32[1,128]{1,0:T(1,128)S(1)}) custom-call(bf16[32,4,256]{2,1,0:T(4,128)(2,1)} %x_hbm.1, f32[1,256]{1,0:T(1,128)} %bitcast.14, bf16[32,256]{1,0:T(8,128)(2,1)} %bitcast.12, bf16[32,256]{1,0:T(8,128)(2,1)} %bitcast.13, f32[1,128]{1,0:T(1,128)} %bitcast.15), custom_call_target="tpu_custom_call" | custom-call | tf_op jit(solution)/shard_map/project/pallas_call | solution.py:205
  1.4 0.1 collective-permute-start
  1.4 1.2 %collective-permute-done = bf16[2,32,128]{2,1,0:T(8,128)(2,1)S(1)} collective-permute-done((bf16[2,32,128]{2,1,0:T(8,128)(2,1)S(1)}, bf16[2,32,128]{2,1,0:T(8,128)(2,1)S(1)}, u32[]{:S(2)}, u32[]{:S(2)}) %collective-permute-start) | collective-permute-done | bytes 16416 | tf_op jit(solution)/shard_map/ppermute | solution.py:237
  2.6 2.7 %collective-permute-start.1 = (bf16[64,128]{1,0:T(8,128)(2,1)S(1)}, bf16[64,128]{1,0:T(8,128)(2,1)S(1)}, u32[]{:S(2)}, u32[]{:S(2)}) collective-permute-start(bf16[64,128]{1,0:T(8,128)(2,1)S(1)} %get-tuple-element.13), channel_id=1, source_target_pairs={{0,3},{1,2},{2,1},{3,0},{4,7},{5,6},{6,5},{7,4},{8,11},{9,10},{10,... | collective-permute-start | bytes 49160 | tf_op jit(solution)/shard_map/ppermute | solution.py:235
  5.3 1.4 %collective-permute-done.1 = bf16[64,128]{1,0:T(8,128)(2,1)S(1)} collective-permute-done((bf16[64,128]{1,0:T(8,128)(2,1)S(1)}, bf16[64,128]{1,0:T(8,128)(2,1)S(1)}, u32[]{:S(2)}, u32[]{:S(2)}) %collective-permute-start.1) | collective-permute-done | bytes 16416 | tf_op jit(solution)/shard_map/ppermute | solution.py:235
  6.7 1.8 %collective-permute-start.3 = (bf16[128,128]{1,0:T(8,128)(2,1)S(1)}, bf16[128,128]{1,0:T(8,128)(2,1)S(1)}, u32[]{:S(2)}, u32[]{:S(2)}) collective-permute-start(bf16[128,128]{1,0:T(8,128)(2,1)S(1)} %pad_maximum_fusion.own_ref), channel_id=1, source_target_pairs={{0,8},{1,4},{2,10},{3,6},{4,12},{5,0},{6,14},{7,2},{8,13},{9,5},{1... | collective-permute-start | bytes 98312 | tf_op jit(solution)/shard_map/ppermute | solution.py:235
  8.5 0.1 turn.1.left_t_ref
  8.6 1.5 %collective-permute-start.2 = (bf16[128,128]{1,0:T(8,128)(2,1)S(1)}, bf16[128,128]{1,0:T(8,128)(2,1)S(1)}, u32[]{:S(2)}, u32[]{:S(2)}) collective-permute-start(bf16[128,128]{1,0:T(8,128)(2,1)S(1)} %pad_maximum_fusion.own_ref), channel_id=1, source_target_pairs={{0,12},{1,0},{2,14},{3,2},{4,8},{5,4},{6,10},{7,6},{8,9},{9,1},{10... | collective-permute-start | bytes 98312 | tf_op jit(solution)/shard_map/ppermute | solution.py:235
  10.1 1.6 %collective-permute-done.3.one_ref = bf16[128,128]{1,0:T(8,128)(2,1)S(1)} collective-permute-done((bf16[128,128]{1,0:T(8,128)(2,1)S(1)}, bf16[128,128]{1,0:T(8,128)(2,1)S(1)}, u32[]{:S(2)}, u32[]{:S(2)}) %collective-permute-start.3) | collective-permute-done | bytes 32800 | tf_op jit(solution)/shard_map/ppermute | solution.py:235
  11.6 0.0 copy-done
  11.6 0.4 %early.1 = (bf16[4,16,128]{2,1,0:T(8,128)(2,1)}, f32[64,128]{1,0:T(8,128)S(1)}) custom-call(s32[1]{0:T(128)} %bitcast.home_ref, s32[1]{0:T(128)} %bitcast.8.low_ref, s32[1]{0:T(128)} %bitcast.9.one_at_ref, bf16[128,64]{1,0:T(8,128)(2,1)S(1)} %turn.1.left_t_ref, bf16[128,128]{1,0:T(8,128)(2,1)S(1)} %pad_maximum_fusion.own_ref, ...), custom_call_target="tpu_custom_call" | custom-call | flops 1000000000 | tf_op jit(solution)/shard_map/early/pallas_call | solution.py:285
  12.1 0.3 %collective-permute-done.2.two_ref = bf16[128,128]{1,0:T(8,128)(2,1)S(1)} collective-permute-done((bf16[128,128]{1,0:T(8,128)(2,1)S(1)}, bf16[128,128]{1,0:T(8,128)(2,1)S(1)}, u32[]{:S(2)}, u32[]{:S(2)}) %collective-permute-start.2) | collective-permute-done | bytes 32800 | tf_op jit(solution)/shard_map/ppermute | solution.py:235
  12.3 1.0 %late.1 = bf16[4,16,128]{2,1,0:T(8,128)(2,1)} custom-call(s32[1]{0:T(128)} %bitcast.home_ref, s32[1]{0:T(128)} %bitcast.1.two_at_ref, bf16[128,64]{1,0:T(8,128)(2,1)S(1)} %turn.1.left_t_ref, bf16[128,128]{1,0:T(8,128)(2,1)S(1)} %collective-permute-done.2.two_ref, bf16[1024,128]{1,0:T(8,128)(2,1)S(1)} %copy-done, ...), custom_call_target="tpu_custom_call", output_to_operand_aliasing={{}: (7, {})} | custom-call | tf_op jit(solution)/shard_map/late/pallas_call | solution.py:294
  (3 shorter events, 0.0 us)
Async XLA Ops:
  0.0 11.6 %copy-start = (bf16[1024,128]{1,0:T(8,128)(2,1)S(1)}, bf16[1024,128]{1,0:T(8,128)(2,1)}, u32[]{:S(2)}) copy-start(bf16[1024,128]{1,0:T(8,128)(2,1)} %weight_ref.3) | copy-start | bytes 786436
  1.4 1.2 %collective-permute-start = (bf16[2,32,128]{2,1,0:T(8,128)(2,1)S(1)}, bf16[2,32,128]{2,1,0:T(8,128)(2,1)S(1)}, u32[]{:S(2)}, u32[]{:S(2)}) collective-permute-start(bf16[2,32,128]{2,1,0:T(8,128)(2,1)S(1)} %get-tuple-element.9), channel_id=1, source_target_pairs={{0,1},{1,0},{2,3},{3,2},{4,5},{5,4},{6,7},{7,6},{8,9},{9,8},{10,11... | collective-permute-start | bytes 49160 | tf_op jit(solution)/shard_map/ppermute | solution.py:237
  2.6 4.1 %collective-permute-start.1 = (bf16[64,128]{1,0:T(8,128)(2,1)S(1)}, bf16[64,128]{1,0:T(8,128)(2,1)S(1)}, u32[]{:S(2)}, u32[]{:S(2)}) collective-permute-start(bf16[64,128]{1,0:T(8,128)(2,1)S(1)} %get-tuple-element.13), channel_id=1, source_target_pairs={{0,3},{1,2},{2,1},{3,0},{4,7},{5,6},{6,5},{7,4},{8,11},{9,10},{10,... | collective-permute-start | bytes 49160 | tf_op jit(solution)/shard_map/ppermute | solution.py:235
  6.7 4.9 %collective-permute-start.3 = (bf16[128,128]{1,0:T(8,128)(2,1)S(1)}, bf16[128,128]{1,0:T(8,128)(2,1)S(1)}, u32[]{:S(2)}, u32[]{:S(2)}) collective-permute-start(bf16[128,128]{1,0:T(8,128)(2,1)S(1)} %pad_maximum_fusion.own_ref), channel_id=1, source_target_pairs={{0,8},{1,4},{2,10},{3,6},{4,12},{5,0},{6,14},{7,2},{8,13},{9,5},{1... | collective-permute-start | bytes 98312 | tf_op jit(solution)/shard_map/ppermute | solution.py:235
  8.6 3.7 %collective-permute-start.2 = (bf16[128,128]{1,0:T(8,128)(2,1)S(1)}, bf16[128,128]{1,0:T(8,128)(2,1)S(1)}, u32[]{:S(2)}, u32[]{:S(2)}) collective-permute-start(bf16[128,128]{1,0:T(8,128)(2,1)S(1)} %pad_maximum_fusion.own_ref), channel_id=1, source_target_pairs={{0,12},{1,0},{2,14},{3,2},{4,8},{5,4},{6,10},{7,6},{8,9},{9,1},{10... | collective-permute-start | bytes 98312 | tf_op jit(solution)/shard_map/ppermute | solution.py:235
